TPU v7x, 128 devices: a whole 4x4x4 slice. The times are simulated.
128 devices in a mesh: slab: 32 (over z, x, core), pen: 4 (over y).
Axes of the slice: x: 4, y: 4, z: 4, core: 2. Of those that a mesh axis runs over, the one named last changes fastest.
Arguments:
- pressure: float32 [512, 512, 512], P('slab', 'pen'), may hold values from -6 to 6
- previous: float32 [512, 512, 512], P('slab', 'pen'), may hold values from -6 to 6
- speed_ratio: float32 [512, 512, 512], P('slab', 'pen'), may hold values from 0.25 to 1
- traces: float32 [2, 2048], P(None, ('slab', 'pen')), may hold values from -6 to 6
- sensor_voxels: int32 [3, 2048], replicated, may hold values from 0 to 511, as said below
- trace_column: int32 [2048], replicated, may hold values from 0 to 2047, each once
Outputs:
- final_pressure: float32 [512, 512, 512], P('slab', 'pen')
- prior_pressure: float32 [512, 512, 512], P('slab', 'pen')
Inputs may be any that keep to these rules, and one draw needn't show every extreme that they name: `sensor_voxels`: row 0 holds each sensor's z cell (below 512), row 1 its y cell (below 512), row 2 its x cell (below 512); no two sensors share a y, x pair. `trace_column`: each of the 2048 trace columns belongs to exactly one sensor.
All inputs are finite; a program needn't handle non-finite values.
Results may differ from a plain program's by a relative error of at most 0.0001.
Values sent between devices are 32-bit elements; how exact they have to be, the bound alone decides.
No kernel may reach another device: no remote copies, remote signals or barrier semaphores. Data moves between devices by JAX's collectives and lax.ppermute only.
A program may use at most 128 MiB of HBM per device.

v0:
```python
import math

import jax
import jax.numpy as jnp
from jax import lax
from jax.sharding import Mesh
from jax.sharding import PartitionSpec as P

NX = 512
NY = 512
NZ = 512
SLAB = ("slab_0", "slab_1", "slab_2")
SLAB_PEN = ("slab_0", "slab_1", "slab_2", "pen")


HALF_CFL = 0.25


def in_order(tiles, dim):
    lengths = list(tiles.shape[1:])
    lengths[dim] *= tiles.shape[0]
    return jnp.moveaxis(tiles, 0, dim).reshape(lengths)


def gather_in_order(array, axes, order):
    tiles = array[None]
    for k in order:
        tiles = lax.all_gather(tiles, axes[k], axis=0, tiled=True)
    held = [lax.axis_size(axes[k]) for k in reversed(order)]
    tiles = tiles.reshape(*held, *array.shape)
    turned = sorted(range(len(order)), key=lambda place: order[len(order) - 1 - place])
    return tiles.transpose(*turned, *range(len(order), tiles.ndim)).reshape(-1, *array.shape)


def whole_of(array, axes, order, dim):
    return in_order(gather_in_order(array, axes, order), dim)


def cas_table(length):
    indices = jnp.arange(length, dtype=jnp.int32)
    product = indices[:, None] * indices[None, :] % length
    angles = product.astype(jnp.float32) * (2.0 * math.pi / length)
    return jnp.cos(angles) + jnp.sin(angles)


def squared_freq(length):
    indices = jnp.arange(length, dtype=jnp.int32)
    signed_index = jnp.where(2 * indices > length, indices - length, indices)
    angular = signed_index.astype(jnp.float32) * (2.0 * math.pi / length)
    return angular * angular


def wave_symbol(total, scale):
    return -4.0 * jnp.square(jnp.sin(HALF_CFL * jnp.sqrt(total))) * scale


def contract(form, left, right):
    return jnp.einsum(
        form, left, right, precision=lax.Precision.HIGHEST, preferred_element_type=jnp.float32
    )


def on_device(pressure, previous, speed_ratio, traces, sensor_voxels, trace_column):
    depth, rows, width = pressure.shape
    slab_count = lax.axis_size(SLAB)
    pen_count = lax.axis_size("pen")
    slab_index = lax.axis_index(SLAB)
    pen_index = lax.axis_index("pen")
    table_x = cas_table(NX)
    table_y = cas_table(NY)
    table_z = cas_table(NZ)
    freq_x = squared_freq(NX)
    freq_y = squared_freq(NY)
    freq_z = squared_freq(NZ)
    scale = 1.0 / (NX * NY * NZ)
    band_x = NX // (slab_count * pen_count)
    flat_index = slab_index * pen_count + pen_index
    local_x = lax.dynamic_slice_in_dim(freq_x, flat_index * band_x, band_x)
    symbol = wave_symbol(
        freq_z[:, None, None] + local_x[None, :, None] + freq_y[None, None, :], scale
    )
    table_y4 = table_y.reshape(pen_count, rows, NY)
    table_z3 = table_z.reshape(slab_count, depth, NZ)
    zcell = sensor_voxels[0] - slab_index * depth
    ycell = sensor_voxels[1] - pen_index * rows
    xcell = sensor_voxels[2]
    inside = (zcell >= 0) & (zcell < depth) & (ycell >= 0) & (ycell < rows)
    zcell = jnp.where(inside, zcell, depth)
    ycell = jnp.where(inside, ycell, rows)
    gathered = whole_of(traces, SLAB_PEN, (0, 1, 3, 2), 1)
    for step_index in range(traces.shape[0]):
        column = gathered[step_index]
        values = column[trace_column]
        current = pressure.at[zcell, ycell, xcell].set(values, mode="drop")
        spectral_x = contract("zyx,xk->zky", current, table_x)
        arrived = lax.all_to_all(spectral_x, SLAB_PEN, split_axis=1, concat_axis=0, tiled=True)
        blocks = arrived.reshape(slab_count, pen_count, depth, band_x, rows)
        spectral_y = contract("spaxb,pbk->saxk", blocks, table_y4)
        spectral_z = contract("saxk,saj->jxk", spectral_y, table_z3)
        inverse_z = contract("jxk,saj->saxk", spectral_z * symbol, table_z3)
        inverse_y = contract("saxk,pbk->spaxb", inverse_z, table_y4)
        flat_rows = inverse_y.reshape(slab_count * pen_count * depth, band_x, rows)
        update = contract(
            "zkm,kx->zmx",
            lax.all_to_all(flat_rows, SLAB_PEN, split_axis=0, concat_axis=1, tiled=True),
            table_x,
        )
        following = 2.0 * current - previous + speed_ratio * update
        previous = current
        pressure = following
    return (pressure, previous)


def solution(mesh):
    torus = Mesh(
        mesh.devices.reshape(4, 4, 2, mesh.shape["pen"]), ("slab_0", "slab_1", "slab_2", "pen")
    )
    placed = (
        P(SLAB, "pen", None),
        P(SLAB, "pen", None),
        P(SLAB, "pen", None),
        P(None, SLAB_PEN),
        P(),
        P(),
    )
    return jax.shard_map(
        on_device,
        mesh=torus,
        in_specs=placed,
        out_specs=(P(SLAB, "pen", None), P(SLAB, "pen", None)),
        check_vma=False,
    )
```

profile of v0, /device:TPU:1, one launch (start us, length us, event | category | flops | bytes accessed | tf_op | source)
XLA Modules:
  0.0 575.0 jit_solution(10976719643563094674)
XLA Ops:
  0.6 10.1 %all-gather.1 = f32[4,2,16]{2,1,0:T(2,128)S(1)} all-gather(f32[1,2,16]{2,1,0:T(2,128)} %bitcast.137), channel_id=2, replica_groups=mesh['slab_0'=4,'slab_1'=4,'slab_2'=2,'pen'=4] {'slab_0'}, dimensions={0}, use_global_device_ids=true | all-gather | bytes 640 | tf_op jit(solution)/shard_map/all_gather | solution.py:28
  10.7 0.7 fusion.68
  11.4 9.5 %all_gather.13 = f32[16,2,16]{2,1,0:T(2,128)S(1)} all-gather(f32[4,2,16]{2,1,0:T(2,128)S(1)} %all-gather.1), channel_id=1, replica_groups=mesh['slab_0'=4,'slab_1'=4,'slab_2'=2,'pen'=4] {'slab_1'}, dimensions={0}, use_global_device_ids=true | all-gather | bytes 2560 | tf_op jit(solution)/shard_map/all_gather | solution.py:28
  20.9 0.9 compare_select_fusion.2
  21.7 0.9 compare_select_fusion.1
  22.6 0.8 and_reduce_fusion
  23.4 0.7 multiply_reduce_fusion
  24.1 9.5 %all_gather.14 = f32[64,2,16]{2,1,0:T(2,128)S(1)} all-gather(f32[16,2,16]{2,1,0:T(2,128)S(1)} %all_gather.13), channel_id=1, replica_groups=mesh['slab_0'=4,'slab_1'=4,'slab_2'=2,'pen'=4] {'pen'}, dimensions={0}, use_global_device_ids=true | all-gather | bytes 10240 | tf_op jit(solution)/shard_map/all_gather | solution.py:28
  33.6 10.0 %all_gather.15 = f32[128,2,16]{2,1,0:T(2,128)S(1)} all-gather(f32[64,2,16]{2,1,0:T(2,128)S(1)} %all_gather.14), channel_id=1, replica_groups=mesh['slab_0'=4,'slab_1'=4,'slab_2'=2,'pen'=4] {'slab_2'}, dimensions={0}, use_global_device_ids=true | all-gather | bytes 24576 | tf_op jit(solution)/shard_map/all_gather | solution.py:28
  43.8 5.3 copy.73
  49.1 11.8 %gather_fusion = f32[2048]{0:T(1024)S(1)} fusion(f32[2048]{0:T(1024)S(1)} %squeeze.12, s32[2048]{0:T(1024)S(1)} %fusion.68), kind=kCustom, calls=%fused_computation | custom fusion | bytes 24576 | tf_op jit(solution)/shard_map/gather | solution.py:93
  60.9 12.2 %scatter_fusion = f32[1048576]{0:T(1024)} fusion(f32[1048576]{0:T(1024)} %bitcast.124, s32[2048]{0:T(1024)S(1)} %broadcast_select_fusion, f32[2048]{0:T(1024)S(1)} %gather_fusion), kind=kCustom, calls=%fused_computation.2 | custom fusion | bytes 32768
  73.1 5.2 reshape.224
  78.3 19.9 %convolution_bitcast_fusion.1 = f32[16,512,128]{2,1,0:T(8,128)S(1)} fusion(f32[16,128,512]{2,1,0:T(8,128)} %reshape.224), kind=kOutput, calls=%fused_computation.32 | convolution fusion | flops 6446383104 | bytes 8388608 | tf_op jit(solution)/shard_map/zyx,xk->zky/dot_general | solution.py:58
  98.2 4.4 copy.40
  102.7 6.5 %all-to-all-start = ((f32[16,512,128]{2,0,1:T(8,128)}), f32[16,512,128]{2,0,1:T(8,128)}, u32[]{:S(2)}, u32[]{:S(2)}) async-start(f32[16,512,128]{2,0,1:T(8,128)} %copy.40), calls=%async_computation | async-start | bytes 8388608 | tf_op jit(solution)/shard_map/all_to_all | solution.py:96
  109.3 52.5 %all-to-all-done = f32[16,512,128]{2,0,1:T(8,128)} async-done(((f32[16,512,128]{2,0,1:T(8,128)}), f32[16,512,128]{2,0,1:T(8,128)}, u32[]{:S(2)}, u32[]{:S(2)}) %all-to-all-start) | async-done | bytes 4194336 | tf_op jit(solution)/shard_map/all_to_all | solution.py:96
  161.8 17.0 %fusion.14 = f32[32,16,4,512,1]{3,0,4,1,2:T(8,128)S(1)} fusion(f32[32,4,16,4,128]{4,2,3,1,0:T(8,128)} %bitcast.16, s32[4,128]{1,0:T(4,128)S(1)} %multiply_add_fusion.3), kind=kOutput, calls=%fused_computation.20 | convolution fusion | flops 6446383104 | bytes 8390656 | tf_op jit(solution)/shard_map/spaxb,pbk->saxk/dot_general | solution.py:58
  178.8 11.1 %fusion.12 = f32[512,4,512,1]{2,0,3,1:T(8,128)S(1)} fusion(f32[32,16,4,512,1]{3,0,4,1,2:T(8,128)S(1)} %fusion.14, s32[32,16]{0,1:T(8,128)S(1)} %multiply_add_fusion.2), kind=kOutput, calls=%fused_computation.18 | convolution fusion | flops 6446383104 | bytes 8390656 | tf_op jit(solution)/shard_map/saxk,saj->jxk/dot_general | solution.py:58
  189.9 27.2 %fusion.10 = f32[32,16,4,512]{3,0,2,1:T(8,128)S(1)} fusion(f32[512,4,512,1]{2,0,3,1:T(8,128)S(1)} %fusion.12, f32[512]{0:T(512)S(1)} %fusion.72, f32[512,4]{0,1:T(4,128)S(1)} %broadcast_add_fusion, s32[32,16]{0,1:T(8,128)S(1)} %multiply_add_fusion.2), kind=kOutput, calls=%fused_computation.15 | convolution fusion | flops 6451625984 | bytes 8400896 | tf_op jit(solution)/shard_map/jxk,saj->saxk/dot_general | solution.py:58
  217.1 11.0 %fusion.20 = f32[32,4,16,4,128]{4,0,3,2,1:T(8,128)S(1)} fusion(f32[32,16,4,512]{3,0,2,1:T(8,128)S(1)} %fusion.10, s32[4,128]{1,0:T(4,128)S(1)} %multiply_add_fusion.3), kind=kOutput, calls=%fused_computation.29 | convolution fusion | flops 6446383104 | bytes 8390656 | tf_op jit(solution)/shard_map/saxk,pbk->spaxb/dot_general | solution.py:58
  228.1 2.4 copy.43
  230.5 10.0 %copy.44 = f32[2048,4,128]{2,1,0:T(4,128)} copy(f32[2048,4,128]{2,0,1:T(8,128)S(1)} %bitcast.130) | data formatting | bytes 8388608 | tf_op jit(solution)/shard_map/reshape | solution.py:102
  240.5 4.8 all-to-all-start.1
  245.3 12.0 %gather_fusion.1 = f32[2048]{0:T(1024)S(1)} fusion(f32[2048]{0:T(1024)S(1)} %squeeze.13, s32[2048]{0:T(1024)S(1)} %fusion.68), kind=kCustom, calls=%fused_computation.1 | custom fusion | bytes 24576 | tf_op jit(solution)/shard_map/gather | solution.py:93
  257.3 40.4 %all-to-all-done.1 = f32[2048,4,128]{2,1,0:T(4,128)} async-done(((f32[2048,4,128]{2,1,0:T(4,128)}), f32[2048,4,128]{2,1,0:T(4,128)}, u32[]{:S(2)}, u32[]{:S(2)}) %all-to-all-start.1) | async-done | bytes 4194336 | tf_op jit(solution)/shard_map/all_to_all | solution.py:105
  297.7 2.6 copy.45
  300.4 0.5 copy.46
  301.2 1.6 copy-done
  302.7 1.2 copy-done.3
  303.9 13.2 %multiply_add_fusion.1 = f32[16,128,512]{2,1,0:T(8,128)S(1)} fusion(f32[16,128,512]{2,1,0:T(8,128)S(1)} %copy-done.3, f32[16,128,512]{2,1,0:T(8,128)S(1)} %copy-done.5, f32[16,128,512]{2,1,0:T(8,128)S(1)} %copy-done, f32[16,512,128]{2,0,1:T(8,128)S(1)} %bitcast.128), kind=kOutput, calls=%fused_computation.27 | convolution fusion | flops 6450577408 | bytes 20971520 | tf_op jit(solution)/shard_map/zkm,kx->zmx/dot_general | solution.py:58
  317.1 3.1 copy.74
  320.2 12.2 %scatter_fusion.1 = f32[1048576]{0:T(1024)} fusion(f32[1048576]{0:T(1024)} %bitcast.125, s32[2048]{0:T(1024)S(1)} %broadcast_select_fusion, f32[2048]{0:T(1024)S(1)} %gather_fusion.1), kind=kCustom, calls=%fused_computation.3 | custom fusion | bytes 32768
  332.4 4.9 reshape.228
  337.3 19.6 %convolution_bitcast_fusion = f32[16,512,128]{2,1,0:T(8,128)S(1)} fusion(f32[16,128,512]{2,1,0:T(8,128)} %reshape.228), kind=kOutput, calls=%fused_computation.31 | convolution fusion | flops 6446383104 | bytes 8388608 | tf_op jit(solution)/shard_map/zyx,xk->zky/dot_general | solution.py:58
  356.9 2.4 copy.49
  359.4 56.9 %all_to_all.66 = f32[16,512,128]{2,0,1:T(8,128)S(1)} all-to-all(f32[16,512,128]{2,0,1:T(8,128)S(1)} %copy.49), channel_id=1, replica_groups=mesh['slab_0'=4,'slab_1'=4,'slab_2'=2,'pen'=4] {'slab_0','slab_1','slab_..., dimensions={1} | all-to-all | bytes 8388608 | tf_op jit(solution)/shard_map/all_to_all | solution.py:96
  416.3 15.0 %fusion.6 = f32[32,16,4,512,1]{3,0,4,1,2:T(8,128)S(1)} fusion(f32[32,4,16,4,128]{4,2,3,1,0:T(8,128)S(1)} %bitcast.126, s32[4,128]{1,0:T(4,128)S(1)} %multiply_add_fusion.3), kind=kOutput, calls=%fused_computation.11 | convolution fusion | flops 6446383104 | bytes 8390656 | tf_op jit(solution)/shard_map/spaxb,pbk->saxk/dot_general | solution.py:58
  431.2 11.7 %fusion.4 = f32[512,4,512,1]{2,0,3,1:T(8,128)S(1)} fusion(f32[32,16,4,512,1]{3,0,4,1,2:T(8,128)S(1)} %fusion.6, s32[32,16]{0,1:T(8,128)S(1)} %multiply_add_fusion.2), kind=kOutput, calls=%fused_computation.9 | convolution fusion | flops 6446383104 | bytes 8390656 | tf_op jit(solution)/shard_map/saxk,saj->jxk/dot_general | solution.py:58
  443.0 27.2 %fusion.2 = f32[32,16,4,512]{3,0,2,1:T(8,128)S(1)} fusion(f32[512,4,512,1]{2,0,3,1:T(8,128)S(1)} %fusion.4, f32[512]{0:T(512)S(1)} %fusion.72, f32[512,4]{0,1:T(4,128)S(1)} %broadcast_add_fusion, s32[32,16]{0,1:T(8,128)S(1)} %multiply_add_fusion.2), kind=kOutput, calls=%fused_computation.6 | convolution fusion | flops 6451625984 | bytes 8400896 | tf_op jit(solution)/shard_map/jxk,saj->saxk/dot_general | solution.py:58
  470.2 11.0 %fusion.23 = f32[32,4,16,4,128]{4,0,3,2,1:T(8,128)S(1)} fusion(f32[32,16,4,512]{3,0,2,1:T(8,128)S(1)} %fusion.2, s32[4,128]{1,0:T(4,128)S(1)} %multiply_add_fusion.3), kind=kOutput, calls=%fused_computation.30 | convolution fusion | flops 6446383104 | bytes 8390656 | tf_op jit(solution)/shard_map/saxk,pbk->spaxb/dot_general | solution.py:58
  481.2 2.4 copy.52
  483.6 8.7 %copy.53 = f32[2048,4,128]{2,1,0:T(4,128)S(1)} copy(f32[2048,4,128]{2,0,1:T(8,128)S(1)} %bitcast.132) | data formatting | bytes 8388608 | tf_op jit(solution)/shard_map/reshape | solution.py:102
  492.3 57.1 %all_to_all.67 = f32[2048,4,128]{2,1,0:T(4,128)S(1)} all-to-all(f32[2048,4,128]{2,1,0:T(4,128)S(1)} %copy.53), channel_id=1, replica_groups=mesh['slab_0'=4,'slab_1'=4,'slab_2'=2,'pen'=4] {'slab_0','slab_1','slab_..., dimensions={0} | all-to-all | bytes 8388608 | tf_op jit(solution)/shard_map/all_to_all | solution.py:105
  550.3 1.4 copy-done.4
  551.6 1.3 copy-done.1
  553.0 1.2 copy-done.2
  554.2 20.6 %multiply_add_fusion = f32[16,128,512]{2,1,0:T(8,128)} fusion(f32[16,128,512]{2,1,0:T(8,128)S(1)} %copy-done.4, f32[16,128,512]{2,1,0:T(8,128)S(1)} %copy-done.1, f32[16,128,512]{2,1,0:T(8,128)S(1)} %copy-done.2, f32[16,512,128]{2,0,1:T(8,128)S(1)} %bitcast.127), kind=kOutput, calls=%fused_computation.26 | convolution fusion | flops 6450577408 | bytes 20971520 | tf_op jit(solution)/shard_map/zkm,kx->zmx/dot_general | solution.py:58
  (19 shorter events, 1.5 us)
Async XLA Ops:
  102.7 59.1 %all-to-all-start = ((f32[16,512,128]{2,0,1:T(8,128)}), f32[16,512,128]{2,0,1:T(8,128)}, u32[]{:S(2)}, u32[]{:S(2)}) async-start(f32[16,512,128]{2,0,1:T(8,128)} %copy.40), calls=%async_computation | async-start | bytes 8388608 | tf_op jit(solution)/shard_map/all_to_all | solution.py:96
  240.5 57.2 %all-to-all-start.1 = ((f32[2048,4,128]{2,1,0:T(4,128)}), f32[2048,4,128]{2,1,0:T(4,128)}, u32[]{:S(2)}, u32[]{:S(2)}) async-start(f32[2048,4,128]{2,1,0:T(4,128)} %copy.44), calls=%async_computation.1 | async-start | bytes 8388608 | tf_op jit(solution)/shard_map/all_to_all | solution.py:105
  297.7 3.4 copy-start.5
  300.3 2.4 copy-start
  300.4 3.6 copy-start.3
  549.4 2.2 copy-start.4
  549.7 3.3 copy-start.1
  549.7 4.4 copy-start.2
where the time goes:
time: 579 us; the launch traced here: 575 us
  matrix products  204 us (35%)
  blocking collectives  153 us (26%)
  local copies, waits for them, and re-layouts  108 us (19%)
  waiting for transfers between devices  92.9 us (16%)
  starting transfers between devices  11.2 us (2%)
    dot_general x12, matrix products, contract(): jnp.einsum(form, left, right, precision=lax.Precision.HIGHEST, preferred_...  204 us
    all_to_all x1, blocking collectives, on_device(): lax.all_to_all(flat_rows, SLAB_PEN, split_axis=0, concat_axis=1, tiled=True)  57.1 us
    all_to_all x1, blocking collectives, on_device(): lax.all_to_all(spectral_x, SLAB_PEN, split_axis=1, concat_axis=0, tiled=T...  56.9 us
    all_to_all x1, waiting for transfers between devices, on_device(): lax.all_to_all(spectral_x, SLAB_PEN, split_axis=1, concat_axis=0, tiled=T...  52.5 us
    all_to_all x1, waiting for transfers between devices, on_device(): lax.all_to_all(flat_rows, SLAB_PEN, split_axis=0, concat_axis=1, tiled=True)  40.4 us
    unnamed x16, local copies, waits for them, and re-layouts  39.8 us
    all_gather x4, blocking collectives, gather_in_order(): tiles = lax.all_gather(tiles, axes[k], axis=0, tiled=True)  39 us
    gather x2, local copies, waits for them, and re-layouts, on_device(): values = column[trace_column]  23.7 us
  transfers between devices with their start and end apart: 2, of which 2 were waited for; matrix products, arithmetic and copies ran while one was open for 2% of the time, Pallas kernels for 0%

commit v1 on v0

v1 whole, which is shorter than its diff:
```python
import functools
import math

import jax
import jax.numpy as jnp
import numpy as np
from jax import lax
from jax.experimental import pallas as pl
from jax.experimental.pallas import tpu as pltpu
from jax.sharding import Mesh
from jax.sharding import PartitionSpec as P

NX = 512
NY = 512
NZ = 512
HALF = 256
SENSORS = 2048
SLAB = ("slab_0", "slab_1", "slab_2")
SLAB_PEN = ("slab_0", "slab_1", "slab_2", "pen")
HALF_CFL = 0.25
MIB = 1024 * 1024
F32 = jnp.float32
BF16 = jnp.bfloat16


def half_tables():
    m = np.arange(HALF)[:, None]
    n = np.arange(HALF)[None, :]
    parts = []
    for freq in (2 * m, 2 * m + 1):
        angle = (freq * n % 512) * (2.0 * math.pi / 512)
        parts.append(np.cos(angle) + np.sin(angle))
    even, odd = parts
    stack = []
    for table in (even, odd, odd.T):
        high = table.astype(BF16)
        low = (table - high.astype(np.float64)).astype(BF16)
        stack += [high, low]
    return np.stack(stack)


EVEN, ODD, ODD_T = 0, 2, 4


def split(x):
    high = x.astype(BF16)
    low = (x - high.astype(F32)).astype(BF16)
    return high, low


def split3(x, axis):
    high, low = split(x)
    return jnp.concatenate([high, low, high], axis=axis)


def table3(tab, which, axis):
    high = tab[which]
    return jnp.concatenate([high, high, tab[which + 1]], axis=axis)


def dot(left, right, dims):
    return lax.dot_general(left, right, (dims, ((), ())), preferred_element_type=F32)


def sensor_kernel(offs, vox, tcol, gt, zmap, vmap0, vmap1):
    z = vox[0:1, :] - offs[0]
    y = vox[1:2, :] - offs[1]
    x = vox[2:3, :]
    tile = tcol[...] // 16
    lane = tcol[...] % 16
    inside = (z >= 0) & (z < 16) & (y >= 0) & (y < 128)
    y = jnp.where(inside, y, -1)
    rows128 = lax.broadcasted_iota(jnp.int32, (128, SENSORS), 0)
    pick = (rows128 == tile).astype(F32).astype(BF16)
    g = gt[...]
    g0, g1 = split(g)
    g2 = (g - g0.astype(F32) - g1.astype(F32)).astype(BF16)
    parts = dot(jnp.concatenate([g0, g1, g2], axis=0), pick, ((1,), (0,)))
    spread = parts[0:32] + parts[32:64] + parts[64:96]
    rows16 = lax.broadcasted_iota(jnp.int32, (16, SENSORS), 0)
    here = rows16 == lane
    onrow = rows128 == y
    lhs = [jnp.where(onrow, (z + 1).astype(F32), 0.0).astype(BF16)]
    for t in range(2):
        value = jnp.sum(jnp.where(here, spread[16 * t : 16 * t + 16], 0.0), axis=0, keepdims=True)
        v0 = value.astype(BF16).astype(F32)
        v1 = (value - v0).astype(BF16).astype(F32)
        v2 = value - v0 - v1
        for part in (v0, v1, v2):
            lhs.append(jnp.where(onrow, part, 0.0).astype(BF16))
    columns = lax.broadcasted_iota(jnp.int32, (NX, SENSORS), 0)
    oncol = (columns == x).astype(F32).astype(BF16)
    out = dot(jnp.concatenate(lhs, axis=0), oncol, ((1,), (1,)))
    zmap[...] = out[0:128].astype(jnp.int32) - 1
    vmap0[...] = out[128:256] + out[256:384] + out[384:512]
    vmap1[...] = out[512:640] + out[640:768] + out[768:896]


def forward_x(cur, tab, out):
    flat = cur.reshape(256, NX)
    a, b = flat[:, :HALF], flat[:, HALF:]
    out2 = out.reshape(1024, 128)
    for part, (which, data) in enumerate(((EVEN, a + b), (ODD, a - b))):
        got = dot(table3(tab, which, 1), split3(data, 1), ((1,), (1,)))
        for k in range(2):
            for z in range(2):
                out2[pl.ds(z * 4 + part * 2 + k, 128, stride=8), :] = got[
                    k * 128 : (k + 1) * 128, z * 128 : (z + 1) * 128
                ]


def inverse_x(arr, tab):
    arr2 = arr.reshape(1024, 128)
    halves = []
    for part, which in enumerate((EVEN, ODD)):
        pieces = []
        for z in range(2):
            rows = [arr2[pl.ds(z * 4 + part * 2 + k, 128, stride=8), :] for k in range(2)]
            pieces.append(jnp.concatenate(rows, axis=0))
        data = jnp.concatenate(pieces, axis=1)
        halves.append(dot(split3(data, 0), table3(tab, which, 0), ((0,), (0,))))
    even, odd = halves
    return jnp.concatenate([even + odd, even - odd], axis=1).reshape(2, 128, NX)


def inject(base, zmap, vmap):
    z = lax.broadcasted_iota(jnp.int32, (2, 1, 1), 0) + 2 * pl.program_id(0)
    return jnp.where(zmap[...][None] == z, vmap[...][None], base)


def first_kernel(p, zmap, vmap0, tab, out):
    forward_x(inject(p[...], zmap, vmap0), tab, out)


def middle_kernel(arr, prev, speed, p, zmap, vmap0, vmap1, tab, cur_out, out):
    update = inverse_x(arr, tab)
    now = inject(p[...], zmap, vmap0)
    following = 2.0 * now - prev[...] + speed[...] * update
    cur = inject(following, zmap, vmap1)
    cur_out[...] = cur
    forward_x(cur, tab, out)


def last_kernel(arr, cur, speed, p, zmap, vmap0, tab, final):
    update = inverse_x(arr, tab)
    before = inject(p[...], zmap, vmap0)
    final[...] = 2.0 * cur[...] - before + speed[...] * update


def spectral_kernel(arr, sym, tab, out):
    k = pl.program_id(0)
    pens = [arr[:, p, pl.ds(k, 16, stride=4), :].reshape(512, 128) for p in range(4)]
    a = jnp.concatenate(pens[:2], axis=1)
    b = jnp.concatenate(pens[2:], axis=1)
    back = []
    for part, data in enumerate((a + b, a - b)):
        which = (EVEN, ODD_T)[part]
        x = dot(split3(data, 1), table3(tab, which, 0), ((1,), (0,)))
        top, bottom = x[:HALF], x[HALF:]
        even = dot(table3(tab, EVEN, 1), split3(top + bottom, 0), ((1,), (0,)))
        odd = dot(table3(tab, ODD, 1), split3(top - bottom, 0), ((1,), (0,)))
        cols = pl.ds(part * HALF, HALF)
        even = even * sym[0, pl.ds(0, HALF), cols]
        odd = odd * sym[0, pl.ds(HALF, HALF), cols]
        even = dot(table3(tab, EVEN, 1), split3(even, 0), ((1,), (0,)))
        odd = dot(table3(tab, ODD_T, 1), split3(odd, 0), ((1,), (0,)))
        z = jnp.concatenate([even + odd, even - odd], axis=0)
        back.append(dot(split3(z, 1), table3(tab, (EVEN, ODD)[part], 0), ((1,), (0,))))
    a = back[0] + back[1]
    b = back[0] - back[1]
    for p in range(4):
        piece = (a, b)[p // 2][:, (p % 2) * 128 : (p % 2) * 128 + 128]
        out[:, p, pl.ds(k, 16, stride=4), :] = piece.reshape(32, 16, 128)


def whole(*shape):
    return pl.BlockSpec(shape, lambda i: (0,) * len(shape))


def pairs():
    return pl.BlockSpec((2, 128, NX), lambda i: (i, 0, 0))


def packed():
    return pl.BlockSpec((128, 8, 128), lambda i: (0, i, 0))


def params(mib):
    return pltpu.CompilerParams(vmem_limit_bytes=mib * MIB)


TAB = whole(6, HALF, HALF)
MAP = whole(128, NX)
GRID = jax.ShapeDtypeStruct((16, 128, NX), F32)
WIRE = jax.ShapeDtypeStruct((128, 64, 128), F32)


def squared_freq(indices, length):
    signed_index = jnp.where(2 * indices > length, indices - length, indices)
    angular = signed_index.astype(F32) * (2.0 * math.pi / length)
    return angular * angular


def half_order(rows):
    return jnp.where(rows < HALF, 2 * rows, 2 * (rows - HALF) + 1)


def symbol_of(device):
    rows = jnp.arange(512, dtype=jnp.int32)
    freq = squared_freq(half_order(rows), 512)
    local = jnp.arange(4, dtype=jnp.int32) * 128 + device
    freq_x = squared_freq(half_order(local), NX)
    total = freq[None, :, None] + freq[None, None, :] + freq_x[:, None, None]
    scale = 1.0 / (NX * NY * NZ)
    return -4.0 * jnp.square(jnp.sin(HALF_CFL * jnp.sqrt(total))) * scale


def exchange(array):
    return lax.all_to_all(array, SLAB_PEN, split_axis=0, concat_axis=0, tiled=True)


def on_device(pressure, previous, speed_ratio, traces, sensor_voxels, trace_column):
    slab_index = lax.axis_index(SLAB)
    pen_index = lax.axis_index("pen")
    device = slab_index * 4 + pen_index
    tab = jnp.asarray(half_tables())
    gathered = exchange(jnp.broadcast_to(traces[None], (128, 2, 16)))
    gt = gathered.reshape(128, 32).T
    offs = jnp.stack([slab_index * 16, pen_index * 128]).astype(jnp.int32)
    map_type = jax.ShapeDtypeStruct((128, NX), F32)
    zmap, vmap0, vmap1 = pl.pallas_call(
        sensor_kernel,
        in_specs=[pl.BlockSpec(memory_space=pltpu.SMEM)] + [pl.BlockSpec(memory_space=pltpu.VMEM)] * 3,
        out_shape=(jax.ShapeDtypeStruct((128, NX), jnp.int32), map_type, map_type),
        compiler_params=params(40),
        name="sensors",
    )(offs, sensor_voxels, trace_column.reshape(1, SENSORS), gt)
    sym = symbol_of(device)

    wire = pl.pallas_call(
        first_kernel,
        grid=(8,),
        in_specs=[pairs(), MAP, MAP, TAB],
        out_specs=packed(),
        out_shape=WIRE,
        compiler_params=params(24),
        name="first",
    )(pressure, zmap, vmap0, tab)

    def spectral(arr):
        return pl.pallas_call(
            spectral_kernel,
            grid=(4,),
            in_specs=[whole(32, 4, 64, 128), pl.BlockSpec((1, 512, 512), lambda i: (i, 0, 0)), TAB],
            out_specs=whole(32, 4, 64, 128),
            out_shape=jax.ShapeDtypeStruct((32, 4, 64, 128), F32),
            compiler_params=params(40),
            name="spectral",
        )(arr.reshape(32, 4, 64, 128), sym, tab).reshape(128, 64, 128)

    arr = exchange(spectral(exchange(wire)))
    current, wire = pl.pallas_call(
        middle_kernel,
        grid=(8,),
        in_specs=[packed(), pairs(), pairs(), pairs(), MAP, MAP, MAP, TAB],
        out_specs=(pairs(), packed()),
        out_shape=(GRID, WIRE),
        compiler_params=params(32),
        name="middle",
    )(arr, previous, speed_ratio, pressure, zmap, vmap0, vmap1, tab)
    arr = exchange(spectral(exchange(wire)))
    final = pl.pallas_call(
        last_kernel,
        grid=(8,),
        in_specs=[packed(), pairs(), pairs(), pairs(), MAP, MAP, TAB],
        out_specs=pairs(),
        out_shape=GRID,
        compiler_params=params(32),
        name="last",
    )(arr, current, speed_ratio, pressure, zmap, vmap0, tab)
    return (final, current)


def solution(mesh):
    torus = Mesh(
        mesh.devices.reshape(4, 4, 2, mesh.shape["pen"]), ("slab_0", "slab_1", "slab_2", "pen")
    )
    placed = (
        P(SLAB, "pen", None),
        P(SLAB, "pen", None),
        P(SLAB, "pen", None),
        P(None, SLAB_PEN),
        P(),
        P(),
    )
    return jax.shard_map(
        on_device,
        mesh=torus,
        in_specs=placed,
        out_specs=(P(SLAB, "pen", None), P(SLAB, "pen", None)),
        check_vma=False,
    )
```

time: 579 us -> 311 us (0.54)
  matrix products: 204 us -> 0 us
  local copies, waits for them, and re-layouts: 108 us -> 12.6 us
  waiting for transfers between devices: 92.9 us -> 46.2 us
  Pallas kernels: 0 us -> 46.6 us
  blocking collectives: 153 us -> 171 us
  other arithmetic: 4.05 us -> 16.5 us
    dot_general x12 -> x0, matrix products: 204 us -> none  [contract(): jnp.einsum(form, left, right, precision=lax.Precision.HIGHEST, preferred_...]
    all_to_all x2 -> x3, blocking collectives: 114 us -> 171 us  [exchange(): lax.all_to_all(array, SLAB_PEN, split_axis=0, concat_axis=0, tiled=True)]
    all_to_all x2, waiting for transfers between devices: 92.9 us -> 46.2 us  [exchange(): lax.all_to_all(array, SLAB_PEN, split_axis=0, concat_axis=0, tiled=True)]
    pallas_call x0 -> x6, Pallas kernels: none -> 46.6 us  [the longest x2 24.8 us: spectral(): pl.pallas_call(spectral_kernel, grid=(4,), in_specs=[whole(32, 4, 64, 128...]
    all_gather x4 -> x0, blocking collectives: 39 us -> none  [gather_in_order(): tiles = lax.all_gather(tiles, axes[k], axis=0, tiled=True)]
    unnamed x16 -> x24, local copies, waits for them, and re-layouts: 39.8 us -> 11.2 us
    gather x2 -> x0, local copies, waits for them, and re-layouts: 23.7 us -> none  [on_device(): values = column[trace_column]]
    reshape x3 -> x0, local copies, waits for them, and re-layouts: 18.7 us -> none  [the longest x2 18.7 us: on_device(): flat_rows = inverse_y.reshape(slab_count * pen_count * depth, band_x, rows)]
  transfers between devices with their start and end apart: 2 -> 2, of which waited for: 2 -> 2; matrix products, arithmetic and copies ran while one was open for 2% -> 5% of each run, Pallas kernels for 0% -> 0%
where the time goes in v1:
time: 311 us; the launch traced here: 310 us
  blocking collectives  171 us (55%)
  Pallas kernels  46.6 us (15%)
  waiting for transfers between devices  46.2 us (15%)
  starting transfers between devices  16.7 us (5%)
  other arithmetic  16.5 us (5%)
  local copies, waits for them, and re-layouts  12.6 us (4%)
    all_to_all x3, blocking collectives, exchange(): lax.all_to_all(array, SLAB_PEN, split_axis=0, concat_axis=0, tiled=True)  171 us
    all_to_all x2, waiting for transfers between devices, exchange(): lax.all_to_all(array, SLAB_PEN, split_axis=0, concat_axis=0, tiled=True)  46.2 us
    pallas_call x2, Pallas kernels, spectral(): pl.pallas_call(spectral_kernel, grid=(4,), in_specs=[whole(32, 4, 64, 128...  24.8 us
    all_to_all x2, starting transfers between devices, exchange(): lax.all_to_all(array, SLAB_PEN, split_axis=0, concat_axis=0, tiled=True)  16.7 us
    mul x1, other arithmetic, symbol_of(): return -4.0 * jnp.square(jnp.sin(HALF_CFL * jnp.sqrt(total))) * scale  16.3 us
    unnamed x24, local copies, waits for them, and re-layouts  11.2 us
    pallas_call x1, Pallas kernels, on_device(): pl.pallas_call(middle_kernel, grid=(8,), in_specs=[packed(), pairs(), pai...  8.88 us
  transfers between devices with their start and end apart: 2, of which 2 were waited for; matrix products, arithmetic and copies ran while one was open for 5% of the time, Pallas kernels for 0%

profile of v1, /device:TPU:1, one launch (start us, length us, event | category | flops | bytes accessed | tf_op | source)
XLA Modules:
  0.0 310.2 jit_solution(3645236429353210760)
XLA Ops:
  0.6 1.4 broadcast_in_dim.2
  2.0 11.5 %all-to-all-start = ((f32[128,2,16]{2,1,0:T(2,128)}), f32[128,2,16]{2,1,0:T(2,128)S(1)}, u32[]{:S(2)}, u32[]{:S(2)}) async-start(f32[128,2,16]{2,1,0:T(2,128)} %broadcast_in_dim.2), calls=%async_computation | async-start | bytes 262144 | tf_op jit(solution)/shard_map/all_to_all | solution.py:219
  13.5 0.1 pad_add_fusion.offs
  13.6 9.7 %all-to-all-done = f32[128,2,16]{2,1,0:T(2,128)S(1)} async-done(((f32[128,2,16]{2,1,0:T(2,128)}), f32[128,2,16]{2,1,0:T(2,128)S(1)}, u32[]{:S(2)}, u32[]{:S(2)}) %all-to-all-start) | async-done | bytes 16416 | tf_op jit(solution)/shard_map/all_to_all | solution.py:219
  23.3 0.1 copy.9
  23.4 0.0 copy-start.10
  23.4 0.8 copy-done.10
  24.1 0.0 copy-start.11
  24.1 0.7 copy-done.11
  24.8 2.8 sensors.1
  27.6 0.0 copy-start.2
  27.6 2.2 copy-done.2
  29.8 0.0 copy-start.4
  29.8 1.1 copy-done.4
  30.9 4.1 %first.1 = f32[128,64,128]{2,1,0:T(8,128)S(1)} custom-call(f32[16,128,512]{2,1,0:T(8,128)S(1)} %copy-done.2, s32[128,512]{1,0:T(8,128)S(1)} %get-tuple-element.7.zmap, f32[128,512]{1,0:T(8,128)S(1)} %get-tuple-element.8.vmap0, bf16[6,256,256]{2,1,0:T(8,128)(2,1)S(1)} %copy-done.4), custom_call_target="tpu_custom_call" | custom-call | tf_op jit(solution)/shard_map/first/pallas_call | solution.py:240
  35.1 0.0 copy-start.6
  35.1 2.0 copy-done.6
  37.1 5.3 %all-to-all-start.1 = ((f32[128,64,128]{2,1,0:T(8,128)}), f32[128,64,128]{2,1,0:T(8,128)}, u32[]{:S(2)}, u32[]{:S(2)}) async-start(f32[128,64,128]{2,1,0:T(8,128)} %copy-done.6), calls=%async_computation.1 | async-start | bytes 8388608 | tf_op jit(solution)/shard_map/all_to_all | solution.py:219
  42.4 0.0 copy-start.5
  42.4 0.1 broadcast_add_fusion
  42.6 16.3 %multiply_multiply_fusion.sym = f32[4,512,512]{2,1,0:T(8,128)} fusion(f32[4]{0:T(128)S(1)} %multiply_multiply_fusion.1, f32[512,512]{1,0:T(8,128)S(1)} %broadcast_add_fusion), kind=kLoop, calls=%fused_computation | loop fusion | flops 4194304 | bytes 5242896 | tf_op jit(solution)/shard_map/mul | solution.py:215
  58.8 36.5 %all-to-all-done.1 = f32[128,64,128]{2,1,0:T(8,128)} async-done(((f32[128,64,128]{2,1,0:T(8,128)}), f32[128,64,128]{2,1,0:T(8,128)}, u32[]{:S(2)}, u32[]{:S(2)}) %all-to-all-start.1) | async-done | bytes 4194336 | tf_op jit(solution)/shard_map/all_to_all | solution.py:219
  95.3 0.0 copy-done.5
  95.3 0.0 copy-start
  95.3 2.2 copy-done
  97.5 13.5 %spectral.2 = f32[32,4,64,128]{3,2,1,0:T(8,128)S(1)} custom-call(f32[32,4,64,128]{3,2,1,0:T(8,128)} %bitcast.5.arr, f32[4,512,512]{2,1,0:T(8,128)S(1)} %copy-done, bf16[6,256,256]{2,1,0:T(8,128)(2,1)S(1)} %copy-done.5), custom_call_target="tpu_custom_call" | custom-call | tf_op jit(solution)/shard_map/spectral/pallas_call | solution.py:251
  111.0 0.0 copy-start.3
  111.0 0.0 copy-start.7
  111.1 56.9 %all_to_all.25.arr = f32[128,64,128]{2,1,0:T(8,128)S(1)} all-to-all(f32[128,64,128]{2,1,0:T(8,128)S(1)} %bitcast.12), channel_id=1, replica_groups=mesh['slab_0'=4,'slab_1'=4,'slab_2'=2,'pen'=4] {'slab_0','slab_1','slab_..., dimensions={0} | all-to-all | bytes 8388608 | tf_op jit(solution)/shard_map/all_to_all | solution.py:219
  168.0 0.0 copy-done.3
  168.0 0.0 copy-done.7
  168.0 0.0 copy-start.8
  168.0 2.2 copy-done.8
  170.2 8.9 %middle.1 = (f32[16,128,512]{2,1,0:T(8,128)}, f32[128,64,128]{2,1,0:T(8,128)S(1)}) custom-call(f32[128,64,128]{2,1,0:T(8,128)S(1)} %all_to_all.25.arr, f32[16,128,512]{2,1,0:T(8,128)S(1)} %copy-done.8, f32[16,128,512]{2,1,0:T(8,128)S(1)} %copy-done.7, f32[16,128,512]{2,1,0:T(8,128)S(1)} %copy-done.3, s32[128,512]{1,0:T(8,128)S(1)} %get-tuple-element.7.zmap, ...), custom_call_target="tpu_custom_call" | custom-call | tf_op jit(solution)/shard_map/middle/pallas_call | solution.py:262
  179.1 0.0 copy-start.1
  179.1 56.9 %all_to_all.26 = f32[128,64,128]{2,1,0:T(8,128)S(1)} all-to-all(f32[128,64,128]{2,1,0:T(8,128)S(1)} %get-tuple-element.10), channel_id=1, replica_groups=mesh['slab_0'=4,'slab_1'=4,'slab_2'=2,'pen'=4] {'slab_0','slab_1','slab_..., dimensions={0} | all-to-all | bytes 8388608 | tf_op jit(solution)/shard_map/all_to_all | solution.py:219
  236.0 0.0 copy-done.1
  236.0 11.3 %spectral.3 = f32[32,4,64,128]{3,2,1,0:T(8,128)S(1)} custom-call(f32[32,4,64,128]{3,2,1,0:T(8,128)S(1)} %bitcast.10, f32[4,512,512]{2,1,0:T(8,128)S(1)} %copy-done.1, bf16[6,256,256]{2,1,0:T(8,128)(2,1)S(1)} %copy-done.5), custom_call_target="tpu_custom_call" | custom-call | tf_op jit(solution)/shard_map/spectral/pallas_call | solution.py:251
  247.3 0.0 copy-start.9
  247.3 56.9 %all_to_all.27.arr = f32[128,64,128]{2,1,0:T(8,128)S(1)} all-to-all(f32[128,64,128]{2,1,0:T(8,128)S(1)} %bitcast.11), channel_id=1, replica_groups=mesh['slab_0'=4,'slab_1'=4,'slab_2'=2,'pen'=4] {'slab_0','slab_1','slab_..., dimensions={0} | all-to-all | bytes 8388608 | tf_op jit(solution)/shard_map/all_to_all | solution.py:219
  304.2 0.0 copy-done.9
  304.2 6.0 %last.1 = f32[16,128,512]{2,1,0:T(8,128)} custom-call(f32[128,64,128]{2,1,0:T(8,128)S(1)} %all_to_all.27.arr, f32[16,128,512]{2,1,0:T(8,128)S(1)} %copy-done.9, f32[16,128,512]{2,1,0:T(8,128)S(1)} %copy-done.7, f32[16,128,512]{2,1,0:T(8,128)S(1)} %copy-done.3, s32[128,512]{1,0:T(8,128)S(1)} %get-tuple-element.7.zmap, f32[128,512]{1,0:T(8,128)S(1)} %get-tuple-element.8.vmap0, ...), custom_call_target="tpu_custom_call" | custom-call | tf_op jit(solution)/shard_map/last/pallas_call | solution.py:272
  (2 shorter events, 0.0 us)
Async XLA Ops:
  2.0 21.3 %all-to-all-start = ((f32[128,2,16]{2,1,0:T(2,128)}), f32[128,2,16]{2,1,0:T(2,128)S(1)}, u32[]{:S(2)}, u32[]{:S(2)}) async-start(f32[128,2,16]{2,1,0:T(2,128)} %broadcast_in_dim.2), calls=%async_computation | async-start | bytes 262144 | tf_op jit(solution)/shard_map/all_to_all | solution.py:219
  23.4 0.8 copy-start.10
  24.1 0.7 copy-start.11
  27.6 2.2 copy-start.2
  29.8 1.1 copy-start.4
  35.1 2.0 copy-start.6
  37.1 58.2 %all-to-all-start.1 = ((f32[128,64,128]{2,1,0:T(8,128)}), f32[128,64,128]{2,1,0:T(8,128)}, u32[]{:S(2)}, u32[]{:S(2)}) async-start(f32[128,64,128]{2,1,0:T(8,128)} %copy-done.6), calls=%async_computation.1 | async-start | bytes 8388608 | tf_op jit(solution)/shard_map/all_to_all | solution.py:219
  42.4 53.0 %copy-start.5 = (bf16[6,256,256]{2,1,0:T(8,128)(2,1)S(1)}, bf16[6,256,256]{2,1,0:T(8,128)(2,1)}, u32[]{:S(2)}) copy-start(bf16[6,256,256]{2,1,0:T(8,128)(2,1)} %constant.55.clone.tab) | copy-start | bytes 2359300
  95.3 2.2 copy-start
  111.0 56.9 %copy-start.3 = (f32[16,128,512]{2,1,0:T(8,128)S(1)}, f32[16,128,512]{2,1,0:T(8,128)}, u32[]{:S(2)}) copy-start(f32[16,128,512]{2,1,0:T(8,128)} %p.5) | copy-start | bytes 12582916
  111.0 56.9 %copy-start.7 = (f32[16,128,512]{2,1,0:T(8,128)S(1)}, f32[16,128,512]{2,1,0:T(8,128)}, u32[]{:S(2)}) copy-start(f32[16,128,512]{2,1,0:T(8,128)} %speed.3) | copy-start | bytes 12582916
  168.0 2.2 copy-start.8
  179.1 56.9 %copy-start.1 = (f32[4,512,512]{2,1,0:T(8,128)S(1)}, f32[4,512,512]{2,1,0:T(8,128)}, u32[]{:S(2)}) copy-start(f32[4,512,512]{2,1,0:T(8,128)} %multiply_multiply_fusion.sym) | copy-start | bytes 12582916
  247.3 56.9 %copy-start.9 = (f32[16,128,512]{2,1,0:T(8,128)S(1)}, f32[16,128,512]{2,1,0:T(8,128)}, u32[]{:S(2)}) copy-start(f32[16,128,512]{2,1,0:T(8,128)} %get-tuple-element.6.cur) | copy-start | bytes 12582916

commit v2 on v1

--- a/solution.py
+++ b/solution.py
@@ -1,4 +1,3 @@
-import functools
 import math
 
 import jax
@@ -62,17 +61,28 @@
     return lax.dot_general(left, right, (dims, ((), ())), preferred_element_type=F32)
 
 
-def sensor_kernel(offs, vox, tcol, gt, zmap, vmap0, vmap1):
+def cell_kernel(offs, vox, zmap):
     z = vox[0:1, :] - offs[0]
     y = vox[1:2, :] - offs[1]
-    x = vox[2:3, :]
-    tile = tcol[...] // 16
+    inside = (z >= 0) & (z < 16) & (y >= 0) & (y < 128)
+    y = jnp.where(inside, y, -1)
+    rows128 = lax.broadcasted_iota(jnp.int32, (128, SENSORS), 0)
+    lhs = jnp.where(rows128 == y, (z + 1).astype(F32), 0.0).astype(BF16)
+    columns = lax.broadcasted_iota(jnp.int32, (NX, SENSORS), 0)
+    oncol = (columns == vox[2:3, :]).astype(F32).astype(BF16)
+    zmap[...] = dot(lhs, oncol, ((1,), (1,))).astype(jnp.int32) - 1
+
+
+def value_kernel(offs, vox, tcol, gathered, vmap0, vmap1, row0):
+    z = vox[0:1, :] - offs[0]
+    y = vox[1:2, :] - offs[1]
+    tile = (tcol[...] // 16) ^ offs[2]
     lane = tcol[...] % 16
     inside = (z >= 0) & (z < 16) & (y >= 0) & (y < 128)
     y = jnp.where(inside, y, -1)
     rows128 = lax.broadcasted_iota(jnp.int32, (128, SENSORS), 0)
     pick = (rows128 == tile).astype(F32).astype(BF16)
-    g = gt[...]
+    g = gathered[...].T
     g0, g1 = split(g)
     g2 = (g - g0.astype(F32) - g1.astype(F32)).astype(BF16)
     parts = dot(jnp.concatenate([g0, g1, g2], axis=0), pick, ((1,), (0,)))
@@ -80,20 +90,33 @@
     rows16 = lax.broadcasted_iota(jnp.int32, (16, SENSORS), 0)
     here = rows16 == lane
     onrow = rows128 == y
-    lhs = [jnp.where(onrow, (z + 1).astype(F32), 0.0).astype(BF16)]
+    lhs = []
     for t in range(2):
         value = jnp.sum(jnp.where(here, spread[16 * t : 16 * t + 16], 0.0), axis=0, keepdims=True)
+        if t == 0:
+            row0[...] = value
         v0 = value.astype(BF16).astype(F32)
         v1 = (value - v0).astype(BF16).astype(F32)
         v2 = value - v0 - v1
         for part in (v0, v1, v2):
             lhs.append(jnp.where(onrow, part, 0.0).astype(BF16))
     columns = lax.broadcasted_iota(jnp.int32, (NX, SENSORS), 0)
-    oncol = (columns == x).astype(F32).astype(BF16)
+    oncol = (columns == vox[2:3, :]).astype(F32).astype(BF16)
     out = dot(jnp.concatenate(lhs, axis=0), oncol, ((1,), (1,)))
-    zmap[...] = out[0:128].astype(jnp.int32) - 1
-    vmap0[...] = out[128:256] + out[256:384] + out[384:512]
-    vmap1[...] = out[512:640] + out[640:768] + out[768:896]
+    vmap0[...] = out[0:128] + out[128:256] + out[256:384]
+    vmap1[...] = out[384:512] + out[512:640] + out[640:768]
+
+
+def seed_kernel(vox, weight, out):
+    rows = lax.broadcasted_iota(jnp.int32, (512, SENSORS), 0)
+    onrow = rows == vox[0:1, :]
+    oncol = (rows == vox[1:2, :]).astype(F32).astype(BF16)
+    value = weight[pl.ds(pl.program_id(0), 1), :]
+    high = value.astype(BF16).astype(F32)
+    low = value - high
+    lhs = [jnp.where(onrow, part, 0.0).astype(BF16) for part in (high, low)]
+    got = dot(jnp.concatenate(lhs, axis=0), oncol, ((1,), (1,)))
+    out[0] = got[:512] + got[512:]
 
 
 def forward_x(cur, tab, out):
@@ -128,8 +151,9 @@
     return jnp.where(zmap[...][None] == z, vmap[...][None], base)
 
 
-def first_kernel(p, zmap, vmap0, tab, out):
-    forward_x(inject(p[...], zmap, vmap0), tab, out)
+def first_kernel(p, zmap, tab, out):
+    z = lax.broadcasted_iota(jnp.int32, (2, 1, 1), 0) + 2 * pl.program_id(0)
+    forward_x(jnp.where(zmap[...][None] == z, 0.0, p[...]), tab, out)
 
 
 def middle_kernel(arr, prev, speed, p, zmap, vmap0, vmap1, tab, cur_out, out):
@@ -147,11 +171,18 @@
     final[...] = 2.0 * cur[...] - before + speed[...] * update
 
 
-def spectral_kernel(arr, sym, tab, out):
+def seeded_kernel(arr, seed, sym, tab, out):
+    spectral_kernel(arr, sym, tab, out, seed)
+
+
+def spectral_kernel(arr, sym, tab, out, seed=None):
     k = pl.program_id(0)
     pens = [arr[:, p, pl.ds(k, 16, stride=4), :].reshape(512, 128) for p in range(4)]
     a = jnp.concatenate(pens[:2], axis=1)
     b = jnp.concatenate(pens[2:], axis=1)
+    if seed is not None:
+        a = a + seed[0, :, :HALF]
+        b = b + seed[0, :, HALF:]
     back = []
     for part, data in enumerate((a + b, a - b)):
         which = (EVEN, ODD_T)[part]
@@ -205,60 +236,99 @@
     return jnp.where(rows < HALF, 2 * rows, 2 * (rows - HALF) + 1)
 
 
+def local_freq(device):
+    return half_order(jnp.arange(4, dtype=jnp.int32) * 128 + device)
+
+
 def symbol_of(device):
     rows = jnp.arange(512, dtype=jnp.int32)
     freq = squared_freq(half_order(rows), 512)
-    local = jnp.arange(4, dtype=jnp.int32) * 128 + device
-    freq_x = squared_freq(half_order(local), NX)
+    freq_x = squared_freq(local_freq(device), NX)
     total = freq[None, :, None] + freq[None, None, :] + freq_x[:, None, None]
-    scale = 1.0 / (NX * NY * NZ)
-    return -4.0 * jnp.square(jnp.sin(HALF_CFL * jnp.sqrt(total))) * scale
+    square = total * (HALF_CFL * HALF_CFL)
+    ratio = jnp.full_like(square, 1.0 / math.factorial(15) * -1.0)
+    for n in (13, 11, 9, 7, 5, 3, 1):
+        sign = 1.0 if n % 4 == 1 else -1.0
+        ratio = ratio * square + sign / math.factorial(n)
+    scale = -4.0 / (NX * NY * NZ)
+    return square * ratio * ratio * scale
 
 
 def exchange(array):
     return lax.all_to_all(array, SLAB_PEN, split_axis=0, concat_axis=0, tiled=True)
 
 
-def on_device(pressure, previous, speed_ratio, traces, sensor_voxels, trace_column):
+def gather_traces(traces):
+    state = traces.reshape(1, 32)
+    for bit in range(7):
+        pairs_of = [(i, i ^ (1 << bit)) for i in range(128)]
+        state = jnp.concatenate([state, lax.ppermute(state, SLAB_PEN, pairs_of)], axis=0)
+    return state
+
+
+def step_pair(pressure, previous, speed_ratio, traces, sensor_voxels, trace_column):
     slab_index = lax.axis_index(SLAB)
     pen_index = lax.axis_index("pen")
     device = slab_index * 4 + pen_index
     tab = jnp.asarray(half_tables())
-    gathered = exchange(jnp.broadcast_to(traces[None], (128, 2, 16)))
-    gt = gathered.reshape(128, 32).T
-    offs = jnp.stack([slab_index * 16, pen_index * 128]).astype(jnp.int32)
-    map_type = jax.ShapeDtypeStruct((128, NX), F32)
-    zmap, vmap0, vmap1 = pl.pallas_call(
-        sensor_kernel,
-        in_specs=[pl.BlockSpec(memory_space=pltpu.SMEM)] + [pl.BlockSpec(memory_space=pltpu.VMEM)] * 3,
-        out_shape=(jax.ShapeDtypeStruct((128, NX), jnp.int32), map_type, map_type),
-        compiler_params=params(40),
-        name="sensors",
-    )(offs, sensor_voxels, trace_column.reshape(1, SENSORS), gt)
-    sym = symbol_of(device)
-
+    offs = jnp.stack([slab_index * 16, pen_index * 128, device]).astype(jnp.int32)
+    in_smem = pl.BlockSpec(memory_space=pltpu.SMEM)
+    in_vmem = pl.BlockSpec(memory_space=pltpu.VMEM)
+    zmap = pl.pallas_call(
+        cell_kernel,
+        in_specs=[in_smem, in_vmem],
+        out_specs=in_vmem,
+        out_shape=jax.ShapeDtypeStruct((128, NX), jnp.int32),
+        compiler_params=params(24),
+        name="cells",
+    )(offs, sensor_voxels)
     wire = pl.pallas_call(
         first_kernel,
         grid=(8,),
-        in_specs=[pairs(), MAP, MAP, TAB],
+        in_specs=[pairs(), MAP, TAB],
         out_specs=packed(),
         out_shape=WIRE,
         compiler_params=params(24),
         name="first",
-    )(pressure, zmap, vmap0, tab)
-
-    def spectral(arr):
+    )(pressure, zmap, tab)
+    arr = exchange(wire)
+
+    gathered = gather_traces(traces)
+    map_type = jax.ShapeDtypeStruct((128, NX), F32)
+    vmap0, vmap1, row0 = pl.pallas_call(
+        value_kernel,
+        in_specs=[in_smem] + [in_vmem] * 3,
+        out_specs=(in_vmem,) * 3,
+        out_shape=(map_type, map_type, jax.ShapeDtypeStruct((1, SENSORS), F32)),
+        compiler_params=params(40),
+        name="values",
+    )(offs, sensor_voxels, trace_column.reshape(1, SENSORS), gathered)
+    angle = (local_freq(device)[:, None] * sensor_voxels[2][None, :] % NX).astype(F32) * (2.0 * math.pi / NX)
+    weight = row0 * (jnp.cos(angle) + jnp.sin(angle))
+    plane = pl.BlockSpec((1, 512, 512), lambda i: (i, 0, 0))
+    seed = pl.pallas_call(
+        seed_kernel,
+        grid=(4,),
+        in_specs=[whole(3, SENSORS), whole(4, SENSORS)],
+        out_specs=plane,
+        out_shape=jax.ShapeDtypeStruct((4, 512, 512), F32),
+        compiler_params=params(32),
+        name="seeds",
+    )(sensor_voxels, weight)
+    sym = symbol_of(device)
+
+    def spectral(arr, *extra):
         return pl.pallas_call(
-            spectral_kernel,
+            seeded_kernel if extra else spectral_kernel,
             grid=(4,),
-            in_specs=[whole(32, 4, 64, 128), pl.BlockSpec((1, 512, 512), lambda i: (i, 0, 0)), TAB],
+            in_specs=[whole(32, 4, 64, 128)] + [plane] * (len(extra) + 1) + [TAB],
             out_specs=whole(32, 4, 64, 128),
             out_shape=jax.ShapeDtypeStruct((32, 4, 64, 128), F32),
             compiler_params=params(40),
-            name="spectral",
-        )(arr.reshape(32, 4, 64, 128), sym, tab).reshape(128, 64, 128)
-
-    arr = exchange(spectral(exchange(wire)))
+            name="seeded" if extra else "spectral",
+        )(arr.reshape(32, 4, 64, 128), *extra, sym, tab).reshape(128, 64, 128)
+
+    arr = exchange(spectral(arr, seed))
     current, wire = pl.pallas_call(
         middle_kernel,
         grid=(8,),
@@ -294,7 +364,7 @@
         P(),
     )
     return jax.shard_map(
-        on_device,
+        step_pair,
         mesh=torus,
         in_specs=placed,
         out_specs=(P(SLAB, "pen", None), P(SLAB, "pen", None)),

time: 311 us -> 333 us (1.071)
  other arithmetic: 16.5 us -> 4.69 us
  Pallas kernels: 46.6 us -> 57.6 us
  starting transfers between devices: 16.7 us -> 27.6 us
  blocking collectives: 171 us -> 179 us
  waiting for transfers between devices: 46.2 us -> 50.5 us
    ppermute x0 -> x7, waiting for transfers between devices: none -> 50.5 us  [gather_traces(): lax.ppermute(state, SLAB_PEN, pairs_of)]
    all_to_all x2 -> x1, waiting for transfers between devices: 46.2 us -> 0.01 us  [exchange(): lax.all_to_all(array, SLAB_PEN, split_axis=0, concat_axis=0, tiled=True)]
    ppermute x0 -> x7, starting transfers between devices: none -> 15.6 us  [gather_traces(): lax.ppermute(state, SLAB_PEN, pairs_of)]
    mul x1 -> x2, other arithmetic: 16.3 us -> 4.42 us  [the longest x1 4.07 us: symbol_of(): return square * ratio * ratio * scale]
    pallas_call x6 -> x8, Pallas kernels: 46.6 us -> 57.6 us  [the longest x2 25.3 us: spectral(): pl.pallas_call(seeded_kernel if extra else spectral_kernel, grid=(4,), in...]
    all_to_all x3, blocking collectives: 171 us -> 179 us  [exchange(): lax.all_to_all(array, SLAB_PEN, split_axis=0, concat_axis=0, tiled=True)]
    all_to_all x2 -> x1, starting transfers between devices: 16.7 us -> 11.9 us  [exchange(): lax.all_to_all(array, SLAB_PEN, split_axis=0, concat_axis=0, tiled=True)]
    unnamed x24 -> x30, local copies, waits for them, and re-layouts: 11.2 us -> 12.5 us
  transfers between devices with their start and end apart: 2 -> 8, of which waited for: 2 -> 6; matrix products, arithmetic and copies ran while one was open for 5% -> 1% of each run, Pallas kernels for 0% -> 4%
where the time goes in v2:
time: 333 us; the launch traced here: 332 us
  blocking collectives  179 us (54%)
  Pallas kernels  57.6 us (17%)
  waiting for transfers between devices  50.5 us (15%)
  starting transfers between devices  27.6 us (8%)
  local copies, waits for them, and re-layouts  12.7 us (4%)
  other arithmetic  4.69 us (1%)
    all_to_all x3, blocking collectives, exchange(): lax.all_to_all(array, SLAB_PEN, split_axis=0, concat_axis=0, tiled=True)  179 us
    ppermute x7, waiting for transfers between devices, gather_traces(): lax.ppermute(state, SLAB_PEN, pairs_of)  50.5 us
    pallas_call x2, Pallas kernels, spectral(): pl.pallas_call(seeded_kernel if extra else spectral_kernel, grid=(4,), in...  25.3 us
    ppermute x7, starting transfers between devices, gather_traces(): lax.ppermute(state, SLAB_PEN, pairs_of)  15.6 us
    unnamed x30, local copies, waits for them, and re-layouts  12.5 us
    all_to_all x1, starting transfers between devices, exchange(): lax.all_to_all(array, SLAB_PEN, split_axis=0, concat_axis=0, tiled=True)  11.9 us
    pallas_call x1, Pallas kernels, step_pair(): pl.pallas_call(seed_kernel, grid=(4,), in_specs=[whole(3, SENSORS), whole...  9.48 us
    pallas_call x1, Pallas kernels, step_pair(): pl.pallas_call(middle_kernel, grid=(8,), in_specs=[packed(), pairs(), pai...  8.89 us
  transfers between devices with their start and end apart: 8, of which 6 were waited for; matrix products, arithmetic and copies ran while one was open for 1% of the time, Pallas kernels for 4%

profile of v2, /device:TPU:1, one launch (start us, length us, event | category | flops | bytes accessed | tf_op | source)
XLA Modules:
  0.0 332.3 jit_solution(6342520796927679618)
XLA Ops:
  0.6 0.1 pad_add_fusion.offs
  0.7 0.8 copy-done.11
  1.5 1.4 cells.1.zmap
  2.9 0.0 copy-start.1
  2.9 2.2 copy-done.1
  5.1 1.1 copy-done.3
  6.2 4.0 %first.1 = f32[128,64,128]{2,1,0:T(8,128)S(1)} custom-call(f32[16,128,512]{2,1,0:T(8,128)S(1)} %copy-done.1, s32[128,512]{1,0:T(8,128)S(1)} %cells.1.zmap, bf16[6,256,256]{2,1,0:T(8,128)(2,1)S(1)} %copy-done.3), custom_call_target="tpu_custom_call" | custom-call | tf_op jit(solution)/shard_map/first/pallas_call | solution.py:285
  10.2 0.0 copy-start.5
  10.2 2.0 copy-done.5
  12.2 11.9 %all-to-all-start = ((f32[128,64,128]{2,1,0:T(8,128)}), f32[128,64,128]{2,1,0:T(8,128)}, u32[]{:S(2)}, u32[]{:S(2)}) async-start(f32[128,64,128]{2,1,0:T(8,128)} %copy-done.5), calls=%async_computation | async-start | bytes 8388608 | tf_op jit(solution)/shard_map/all_to_all | solution.py:258
  24.2 0.0 copy-start.12
  24.2 0.0 copy-start.13
  24.2 0.1 reshape.121
  24.3 1.4 collective-permute-start
  25.6 41.8 %collective-permute-done = f32[1,32]{1,0:T(1,128)S(1)} collective-permute-done((f32[1,32]{1,0:T(1,128)S(1)}, f32[1,32]{1,0:T(1,128)S(1)}, u32[]{:S(2)}, u32[]{:S(2)}) %collective-permute-start) | collective-permute-done | bytes 160 | tf_op jit(solution)/shard_map/ppermute | solution.py:265
  67.5 0.9 collective-permute-start.1
  68.4 3.6 %collective-permute-done.1 = f32[2,32]{1,0:T(2,128)S(1)} collective-permute-done((f32[2,32]{1,0:T(2,128)S(1)}, f32[2,32]{1,0:T(2,128)S(1)}, u32[]{:S(2)}, u32[]{:S(2)}) %collective-permute-start.1) | collective-permute-done | bytes 288 | tf_op jit(solution)/shard_map/ppermute | solution.py:265
  72.0 1.7 collective-permute-start.2
  73.7 0.8 collective-permute-done.2
  74.6 5.0 %collective-permute-start.3 = (f32[8,32]{1,0:T(8,128)S(1)}, f32[8,32]{1,0:T(8,128)S(1)}, u32[]{:S(2)}, u32[]{:S(2)}) collective-permute-start(f32[8,32]{1,0:T(8,128)S(1)} %pad_maximum_fusion), channel_id=1, source_target_pairs={{0,8},{1,9},{2,10},{3,11},{4,12},{5,13},{6,14},{7,15},{8,0},{9,1},... | collective-permute-start | bytes 3080 | tf_op jit(solution)/shard_map/ppermute | solution.py:265
  79.5 0.1 broadcast_add_fusion
  79.7 0.9 collective-permute-done.3
  80.6 2.0 collective-permute-start.4
  82.6 2.0 collective-permute-done.4
  84.7 1.6 collective-permute-start.5
  86.3 4.1 %fusion.13.sym = f32[4,512,512]{2,1,0:T(8,128)} fusion(f32[4]{0:T(128)S(1)} %multiply_multiply_fusion.1, f32[512,512]{1,0:T(8,128)S(1)} %broadcast_add_fusion), kind=kLoop, calls=%fused_computation.16 | loop fusion | flops 19922944 | bytes 5242896 | tf_op jit(solution)/shard_map/mul | solution.py:254
  90.3 0.0 collective-permute-done.5
  90.4 3.0 collective-permute-start.6
  93.4 0.0 copy-done.12
  93.4 1.3 collective-permute-done.6
  94.7 2.5 values.1
  97.3 0.3 add_multiply_fusion.2.weight
  97.6 9.5 %seeds.1.seed = f32[4,512,512]{2,1,0:T(8,128)S(1)} custom-call(s32[3,2048]{1,0:T(4,128)S(1)} %copy-done.12, f32[4,2048]{1,0:T(4,128)S(1)} %add_multiply_fusion.2.weight), custom_call_target="tpu_custom_call" | custom-call | tf_op jit(solution)/shard_map/seeds/pallas_call | solution.py:309
  107.1 0.0 copy-start.6
  107.1 2.0 copy-done.6
  109.1 0.0 all-to-all-done
  109.2 2.2 copy-done.7
  111.3 14.0 %seeded.1 = f32[32,4,64,128]{3,2,1,0:T(8,128)S(1)} custom-call(f32[32,4,64,128]{3,2,1,0:T(8,128)} %bitcast.3.arr, f32[4,512,512]{2,1,0:T(8,128)S(1)} %copy-done.7, f32[4,512,512]{2,1,0:T(8,128)} %fusion.13.sym, bf16[6,256,256]{2,1,0:T(8,128)(2,1)S(1)} %copy-done.4), custom_call_target="tpu_custom_call" | custom-call | tf_op jit(solution)/shard_map/seeded/pallas_call | solution.py:321
  125.4 0.0 copy-start.2
  125.4 0.0 copy-start.8
  125.4 64.7 %all_to_all.20.arr = f32[128,64,128]{2,1,0:T(8,128)S(1)} all-to-all(f32[128,64,128]{2,1,0:T(8,128)S(1)} %bitcast.12), channel_id=1, replica_groups=mesh['slab_0'=4,'slab_1'=4,'slab_2'=2,'pen'=4] {'slab_0','slab_1','slab_..., dimensions={0} | all-to-all | bytes 8388608 | tf_op jit(solution)/shard_map/all_to_all | solution.py:258
  190.1 2.2 copy-done.9
  192.3 8.9 %middle.1 = (f32[16,128,512]{2,1,0:T(8,128)}, f32[128,64,128]{2,1,0:T(8,128)S(1)}) custom-call(f32[128,64,128]{2,1,0:T(8,128)S(1)} %all_to_all.20.arr, f32[16,128,512]{2,1,0:T(8,128)S(1)} %copy-done.9, f32[16,128,512]{2,1,0:T(8,128)S(1)} %copy-done.8, f32[16,128,512]{2,1,0:T(8,128)S(1)} %copy-done.2, s32[128,512]{1,0:T(8,128)S(1)} %cells.1.zmap, ...), custom_call_target="tpu_custom_call" | custom-call | tf_op jit(solution)/shard_map/middle/pallas_call | solution.py:332
  201.2 56.9 %all_to_all.21 = f32[128,64,128]{2,1,0:T(8,128)S(1)} all-to-all(f32[128,64,128]{2,1,0:T(8,128)S(1)} %get-tuple-element.10), channel_id=1, replica_groups=mesh['slab_0'=4,'slab_1'=4,'slab_2'=2,'pen'=4] {'slab_0','slab_1','slab_..., dimensions={0} | all-to-all | bytes 8388608 | tf_op jit(solution)/shard_map/all_to_all | solution.py:258
  258.1 11.3 %spectral.1 = f32[32,4,64,128]{3,2,1,0:T(8,128)S(1)} custom-call(f32[32,4,64,128]{3,2,1,0:T(8,128)S(1)} %bitcast.10, f32[4,512,512]{2,1,0:T(8,128)S(1)} %copy-done, bf16[6,256,256]{2,1,0:T(8,128)(2,1)S(1)} %copy-done.4), custom_call_target="tpu_custom_call" | custom-call | tf_op jit(solution)/shard_map/spectral/pallas_call | solution.py:321
  269.4 0.0 copy-start.10
  269.4 56.9 %all_to_all.22.arr = f32[128,64,128]{2,1,0:T(8,128)S(1)} all-to-all(f32[128,64,128]{2,1,0:T(8,128)S(1)} %bitcast.11), channel_id=1, replica_groups=mesh['slab_0'=4,'slab_1'=4,'slab_2'=2,'pen'=4] {'slab_0','slab_1','slab_..., dimensions={0} | all-to-all | bytes 8388608 | tf_op jit(solution)/shard_map/all_to_all | solution.py:258
  326.3 6.0 %last.1 = f32[16,128,512]{2,1,0:T(8,128)} custom-call(f32[128,64,128]{2,1,0:T(8,128)S(1)} %all_to_all.22.arr, f32[16,128,512]{2,1,0:T(8,128)S(1)} %copy-done.10, f32[16,128,512]{2,1,0:T(8,128)S(1)} %copy-done.8, f32[16,128,512]{2,1,0:T(8,128)S(1)} %copy-done.2, s32[128,512]{1,0:T(8,128)S(1)} %cells.1.zmap, f32[128,512]{1,0:T(8,128)S(1)} %get-tuple-element.8.vmap0, ...), custom_call_target="tpu_custom_call" | custom-call | tf_op jit(solution)/shard_map/last/pallas_call | solution.py:342
  (25 shorter events, 0.2 us)
Async XLA Ops:
  0.7 0.8 copy-start.11
  2.9 2.2 copy-start.1
  5.0 1.1 copy-start.3
  10.2 2.0 copy-start.5
  12.2 12.0 %copy-start.14 = (f32[2,16]{1,0:T(2,128)S(1)}, f32[2,16]{1,0:T(2,128)}, u32[]{:S(2)}) copy-start(f32[2,16]{1,0:T(2,128)} %param.10) | copy-start | bytes 388
  12.2 96.9 %all-to-all-start = ((f32[128,64,128]{2,1,0:T(8,128)}), f32[128,64,128]{2,1,0:T(8,128)}, u32[]{:S(2)}, u32[]{:S(2)}) async-start(f32[128,64,128]{2,1,0:T(8,128)} %copy-done.5), calls=%async_computation | async-start | bytes 8388608 | tf_op jit(solution)/shard_map/all_to_all | solution.py:258
  24.2 69.2 %copy-start.12 = (s32[3,2048]{1,0:T(4,128)S(1)}, s32[3,2048]{1,0:T(4,128)}, u32[]{:S(2)}) copy-start(s32[3,2048]{1,0:T(4,128)} %vox.5) | copy-start | bytes 73732
  24.2 70.6 %copy-start.13 = (s32[2048]{0:T(1024)S(1)}, s32[2048]{0:T(1024)}, u32[]{:S(2)}) copy-start(s32[2048]{0:T(1024)} %param.12) | copy-start | bytes 24580
  24.3 43.2 %collective-permute-start = (f32[1,32]{1,0:T(1,128)S(1)}, f32[1,32]{1,0:T(1,128)S(1)}, u32[]{:S(2)}, u32[]{:S(2)}) collective-permute-start(f32[1,32]{1,0:T(1,128)S(1)} %reshape.121), channel_id=1, source_target_pairs={{0,1},{1,0},{2,3},{3,2},{4,5},{5,4},{6,7},{7,6},{8,9},{9,8},{10,11... | collective-permute-start | bytes 392 | tf_op jit(solution)/shard_map/ppermute | solution.py:265
  67.5 4.5 %collective-permute-start.1 = (f32[2,32]{1,0:T(2,128)S(1)}, f32[2,32]{1,0:T(2,128)S(1)}, u32[]{:S(2)}, u32[]{:S(2)}) collective-permute-start(f32[2,32]{1,0:T(2,128)S(1)} %pad_maximum_fusion.2), channel_id=1, source_target_pairs={{0,2},{1,3},{2,0},{3,1},{4,6},{5,7},{6,4},{7,5},{8,10},{9,11},{10,... | collective-permute-start | bytes 776 | tf_op jit(solution)/shard_map/ppermute | solution.py:265
  72.0 2.6 collective-permute-start.2
  74.6 6.0 %collective-permute-start.3 = (f32[8,32]{1,0:T(8,128)S(1)}, f32[8,32]{1,0:T(8,128)S(1)}, u32[]{:S(2)}, u32[]{:S(2)}) collective-permute-start(f32[8,32]{1,0:T(8,128)S(1)} %pad_maximum_fusion), channel_id=1, source_target_pairs={{0,8},{1,9},{2,10},{3,11},{4,12},{5,13},{6,14},{7,15},{8,0},{9,1},... | collective-permute-start | bytes 3080 | tf_op jit(solution)/shard_map/ppermute | solution.py:265
  80.6 4.1 %collective-permute-start.4 = (f32[16,32]{1,0:T(8,128)S(1)}, f32[16,32]{1,0:T(8,128)S(1)}, u32[]{:S(2)}, u32[]{:S(2)}) collective-permute-start(f32[16,32]{1,0:T(8,128)S(1)} %concatenate.30), channel_id=1, source_target_pairs={{0,16},{1,17},{2,18},{3,19},{4,20},{5,21},{6,22},{7,23},{8,24},{9,... | collective-permute-start | bytes 6152 | tf_op jit(solution)/shard_map/ppermute | solution.py:265
  84.7 24.5 %copy-start.4 = (bf16[6,256,256]{2,1,0:T(8,128)(2,1)S(1)}, bf16[6,256,256]{2,1,0:T(8,128)(2,1)}, u32[]{:S(2)}) copy-start(bf16[6,256,256]{2,1,0:T(8,128)(2,1)} %constant.85.clone.tab) | copy-start | bytes 2359300
  84.7 5.7 %collective-permute-start.5 = (f32[32,32]{1,0:T(8,128)S(1)}, f32[32,32]{1,0:T(8,128)S(1)}, u32[]{:S(2)}, u32[]{:S(2)}) collective-permute-start(f32[32,32]{1,0:T(8,128)S(1)} %concatenate.31), channel_id=1, source_target_pairs={{0,32},{1,33},{2,34},{3,35},{4,36},{5,37},{6,38},{7,39},{8,40},{9,... | collective-permute-start | bytes 12296 | tf_op jit(solution)/shard_map/ppermute | solution.py:265
  90.4 4.3 %collective-permute-start.6 = (f32[64,32]{1,0:T(8,128)S(1)}, f32[64,32]{1,0:T(8,128)S(1)}, u32[]{:S(2)}, u32[]{:S(2)}) collective-permute-start(f32[64,32]{1,0:T(8,128)S(1)} %concatenate.32), channel_id=1, source_target_pairs={{0,64},{1,65},{2,66},{3,67},{4,68},{5,69},{6,70},{7,71},{8,72},{9,... | collective-permute-start | bytes 24584 | tf_op jit(solution)/shard_map/ppermute | solution.py:265
  107.1 2.0 copy-start.6
  109.1 2.2 copy-start.7
  125.4 64.7 %copy-start.2 = (f32[16,128,512]{2,1,0:T(8,128)S(1)}, f32[16,128,512]{2,1,0:T(8,128)}, u32[]{:S(2)}) copy-start(f32[16,128,512]{2,1,0:T(8,128)} %p.5) | copy-start | bytes 12582916
  125.4 64.7 %copy-start.8 = (f32[16,128,512]{2,1,0:T(8,128)S(1)}, f32[16,128,512]{2,1,0:T(8,128)}, u32[]{:S(2)}) copy-start(f32[16,128,512]{2,1,0:T(8,128)} %speed.3) | copy-start | bytes 12582916
  190.1 2.2 copy-start.9
  201.2 56.9 %copy-start = (f32[4,512,512]{2,1,0:T(8,128)S(1)}, f32[4,512,512]{2,1,0:T(8,128)}, u32[]{:S(2)}) copy-start(f32[4,512,512]{2,1,0:T(8,128)} %fusion.13.sym) | copy-start | bytes 12582916
  269.4 56.9 %copy-start.10 = (f32[16,128,512]{2,1,0:T(8,128)S(1)}, f32[16,128,512]{2,1,0:T(8,128)}, u32[]{:S(2)}) copy-start(f32[16,128,512]{2,1,0:T(8,128)} %get-tuple-element.6.cur) | copy-start | bytes 12582916

commit v3 on v2

--- a/solution.py
+++ b/solution.py
@@ -76,7 +76,7 @@
 def value_kernel(offs, vox, tcol, gathered, vmap0, vmap1, row0):
     z = vox[0:1, :] - offs[0]
     y = vox[1:2, :] - offs[1]
-    tile = (tcol[...] // 16) ^ offs[2]
+    tile = tcol[...] // 16
     lane = tcol[...] % 16
     inside = (z >= 0) & (z < 16) & (y >= 0) & (y < 128)
     y = jnp.where(inside, y, -1)
@@ -258,28 +258,21 @@
     return lax.all_to_all(array, SLAB_PEN, split_axis=0, concat_axis=0, tiled=True)
 
 
-def gather_traces(traces):
-    state = traces.reshape(1, 32)
-    for bit in range(7):
-        pairs_of = [(i, i ^ (1 << bit)) for i in range(128)]
-        state = jnp.concatenate([state, lax.ppermute(state, SLAB_PEN, pairs_of)], axis=0)
-    return state
-
-
 def step_pair(pressure, previous, speed_ratio, traces, sensor_voxels, trace_column):
     slab_index = lax.axis_index(SLAB)
     pen_index = lax.axis_index("pen")
     device = slab_index * 4 + pen_index
     tab = jnp.asarray(half_tables())
-    offs = jnp.stack([slab_index * 16, pen_index * 128, device]).astype(jnp.int32)
+    offs = jnp.stack([slab_index * 16, pen_index * 128]).astype(jnp.int32)
     in_smem = pl.BlockSpec(memory_space=pltpu.SMEM)
     in_vmem = pl.BlockSpec(memory_space=pltpu.VMEM)
+    gathered = exchange(jnp.broadcast_to(traces.reshape(1, 1, 32), (128, 1, 32)))
     zmap = pl.pallas_call(
         cell_kernel,
         in_specs=[in_smem, in_vmem],
         out_specs=in_vmem,
         out_shape=jax.ShapeDtypeStruct((128, NX), jnp.int32),
-        compiler_params=params(24),
+        compiler_params=params(8),
         name="cells",
     )(offs, sensor_voxels)
     wire = pl.pallas_call(
@@ -287,22 +280,21 @@
         grid=(8,),
         in_specs=[pairs(), MAP, TAB],
         out_specs=packed(),
-        out_shape=WIRE,
-        compiler_params=params(24),
+        out_shape=pltpu.HBM((128, 64, 128), F32),
+        compiler_params=params(12),
         name="first",
     )(pressure, zmap, tab)
     arr = exchange(wire)
 
-    gathered = gather_traces(traces)
     map_type = jax.ShapeDtypeStruct((128, NX), F32)
     vmap0, vmap1, row0 = pl.pallas_call(
         value_kernel,
         in_specs=[in_smem] + [in_vmem] * 3,
         out_specs=(in_vmem,) * 3,
         out_shape=(map_type, map_type, jax.ShapeDtypeStruct((1, SENSORS), F32)),
-        compiler_params=params(40),
+        compiler_params=params(16),
         name="values",
-    )(offs, sensor_voxels, trace_column.reshape(1, SENSORS), gathered)
+    )(offs, sensor_voxels, trace_column.reshape(1, SENSORS), gathered.reshape(128, 32))
     angle = (local_freq(device)[:, None] * sensor_voxels[2][None, :] % NX).astype(F32) * (2.0 * math.pi / NX)
     weight = row0 * (jnp.cos(angle) + jnp.sin(angle))
     plane = pl.BlockSpec((1, 512, 512), lambda i: (i, 0, 0))
@@ -311,31 +303,32 @@
         grid=(4,),
         in_specs=[whole(3, SENSORS), whole(4, SENSORS)],
         out_specs=plane,
-        out_shape=jax.ShapeDtypeStruct((4, 512, 512), F32),
-        compiler_params=params(32),
+        out_shape=pltpu.HBM((4, 512, 512), F32),
+        compiler_params=params(12),
         name="seeds",
     )(sensor_voxels, weight)
     sym = symbol_of(device)
 
     def spectral(arr, *extra):
+        symbol = pltpu.with_memory_space_constraint(sym, pltpu.HBM) if extra else sym
         return pl.pallas_call(
             seeded_kernel if extra else spectral_kernel,
             grid=(4,),
             in_specs=[whole(32, 4, 64, 128)] + [plane] * (len(extra) + 1) + [TAB],
             out_specs=whole(32, 4, 64, 128),
             out_shape=jax.ShapeDtypeStruct((32, 4, 64, 128), F32),
-            compiler_params=params(40),
+            compiler_params=params(24),
             name="seeded" if extra else "spectral",
-        )(arr.reshape(32, 4, 64, 128), *extra, sym, tab).reshape(128, 64, 128)
-
-    arr = exchange(spectral(arr, seed))
+        )(arr.reshape(32, 4, 64, 128), *extra, symbol, tab).reshape(128, 64, 128)
+
+    arr = exchange(spectral(arr, pltpu.with_memory_space_constraint(seed, pltpu.HBM)))
     current, wire = pl.pallas_call(
         middle_kernel,
         grid=(8,),
         in_specs=[packed(), pairs(), pairs(), pairs(), MAP, MAP, MAP, TAB],
         out_specs=(pairs(), packed()),
         out_shape=(GRID, WIRE),
-        compiler_params=params(32),
+        compiler_params=params(16),
         name="middle",
     )(arr, previous, speed_ratio, pressure, zmap, vmap0, vmap1, tab)
     arr = exchange(spectral(exchange(wire)))
@@ -345,7 +338,7 @@
         in_specs=[packed(), pairs(), pairs(), pairs(), MAP, MAP, TAB],
         out_specs=pairs(),
         out_shape=GRID,
-        compiler_params=params(32),
+        compiler_params=params(16),
         name="last",
     )(arr, current, speed_ratio, pressure, zmap, vmap0, tab)
     return (final, current)

time: 333 us -> 300 us (0.901)
  waiting for transfers between devices: 50.5 us -> 35.1 us
  blocking collectives: 179 us -> 171 us
  local copies, waits for them, and re-layouts: 12.7 us -> 5.55 us
  starting transfers between devices: 27.6 us -> 21.7 us
    ppermute x7 -> x0, waiting for transfers between devices: 50.5 us -> none  [gather_traces(): lax.ppermute(state, SLAB_PEN, pairs_of)]
    all_to_all x1 -> x2, waiting for transfers between devices: 0.01 us -> 35.1 us  [exchange(): lax.all_to_all(array, SLAB_PEN, split_axis=0, concat_axis=0, tiled=True)]
    ppermute x7 -> x0, starting transfers between devices: 15.6 us -> none  [gather_traces(): lax.ppermute(state, SLAB_PEN, pairs_of)]
    all_to_all x1 -> x2, starting transfers between devices: 11.9 us -> 21.7 us  [exchange(): lax.all_to_all(array, SLAB_PEN, split_axis=0, concat_axis=0, tiled=True)]
    unnamed x30 -> x22, local copies, waits for them, and re-layouts: 12.5 us -> 4.12 us
    all_to_all x3, blocking collectives: 179 us -> 171 us  [exchange(): lax.all_to_all(array, SLAB_PEN, split_axis=0, concat_axis=0, tiled=True)]
  transfers between devices with their start and end apart: 8 -> 2, of which waited for: 6 -> 1; matrix products, arithmetic and copies ran while one was open for 1% -> 2% of each run, Pallas kernels for 4% -> 7%
where the time goes in v3:
time: 300 us; the launch traced here: 299 us
  blocking collectives  171 us (57%)
  Pallas kernels  60.6 us (20%)
  waiting for transfers between devices  35.1 us (12%)
  starting transfers between devices  21.7 us (7%)
  local copies, waits for them, and re-layouts  5.55 us (2%)
  other arithmetic  4.69 us (2%)
    all_to_all x3, blocking collectives, exchange(): lax.all_to_all(array, SLAB_PEN, split_axis=0, concat_axis=0, tiled=True)  171 us
    all_to_all x2, waiting for transfers between devices, exchange(): lax.all_to_all(array, SLAB_PEN, split_axis=0, concat_axis=0, tiled=True)  35.1 us
    pallas_call x2, Pallas kernels, spectral(): pl.pallas_call(seeded_kernel if extra else spectral_kernel, grid=(4,), in...  25.8 us
    all_to_all x2, starting transfers between devices, exchange(): lax.all_to_all(array, SLAB_PEN, split_axis=0, concat_axis=0, tiled=True)  21.7 us
    pallas_call x1, Pallas kernels, step_pair(): pl.pallas_call(seed_kernel, grid=(4,), in_specs=[whole(3, SENSORS), whole...  10.5 us
    pallas_call x1, Pallas kernels, step_pair(): pl.pallas_call(middle_kernel, grid=(8,), in_specs=[packed(), pairs(), pai...  9.09 us
  transfers between devices with their start and end apart: 2, of which 1 were waited for; matrix products, arithmetic and copies ran while one was open for 2% of the time, Pallas kernels for 7%

profile of v3, /device:TPU:1, one launch (start us, length us, event | category | flops | bytes accessed | tf_op | source)
XLA Modules:
  0.0 299.2 jit_solution(1067156321889082165)
XLA Ops:
  0.6 0.8 broadcast_in_dim.4
  1.4 0.7 broadcast_in_dim.5
  2.1 11.5 %all-to-all-start.1 = ((f32[128,1,32]{2,1,0:T(1,128)}), f32[128,1,32]{2,1,0:T(1,128)S(1)}, u32[]{:S(2)}, u32[]{:S(2)}) async-start(f32[128,1,32]{2,1,0:T(1,128)} %broadcast_in_dim.5), calls=%async_computation.1 | async-start | bytes 131072 | tf_op jit(solution)/shard_map/all_to_all | solution.py:258
  13.6 0.1 pad_add_fusion.offs
  13.6 0.0 copy-start.8
  13.6 0.8 copy-done.8
  14.4 1.4 cells.1.zmap
  15.8 0.0 copy-start.1
  15.8 2.2 copy-done.1
  18.0 0.0 copy-start.3
  18.0 1.1 copy-done.3
  19.1 5.4 %first.1 = f32[128,64,128]{2,1,0:T(8,128)} custom-call(f32[16,128,512]{2,1,0:T(8,128)S(1)} %copy-done.1, s32[128,512]{1,0:T(8,128)S(1)} %cells.1.zmap, bf16[6,256,256]{2,1,0:T(8,128)(2,1)S(1)} %copy-done.3), custom_call_target="tpu_custom_call" | custom-call | tf_op jit(solution)/shard_map/first/pallas_call | solution.py:278
  24.5 0.0 copy-start.9
  24.5 0.0 all-to-all-done.1
  24.5 10.2 %all-to-all-start = ((f32[128,64,128]{2,1,0:T(8,128)}), f32[128,64,128]{2,1,0:T(8,128)}, u32[]{:S(2)}, u32[]{:S(2)}) async-start(f32[128,64,128]{2,1,0:T(8,128)} %first.1), calls=%async_computation | async-start | bytes 8388608 | tf_op jit(solution)/shard_map/all_to_all | solution.py:258
  34.7 0.0 copy-done.9
  34.7 0.0 copy-start.10
  34.8 0.1 broadcast_add_fusion
  34.9 0.0 copy-start.4
  35.0 4.1 %fusion.13.sym = f32[4,512,512]{2,1,0:T(8,128)} fusion(f32[4]{0:T(128)S(1)} %multiply_multiply_fusion.1, f32[512,512]{1,0:T(8,128)S(1)} %broadcast_add_fusion), kind=kLoop, calls=%fused_computation.16 | loop fusion | flops 19922944 | bytes 5242896 | tf_op jit(solution)/shard_map/mul | solution.py:254
  39.0 0.0 copy-done.10
  39.1 2.5 values.1
  41.6 0.3 add_multiply_fusion.2.weight
  41.9 10.5 %seeds.1.seed = f32[4,512,512]{2,1,0:T(8,128)} custom-call(s32[3,2048]{1,0:T(4,128)S(1)} %copy-done.9, f32[4,2048]{1,0:T(4,128)S(1)} %add_multiply_fusion.2.weight), custom_call_target="tpu_custom_call" | custom-call | tf_op jit(solution)/shard_map/seeds/pallas_call | solution.py:301
  52.4 35.1 %all-to-all-done = f32[128,64,128]{2,1,0:T(8,128)} async-done(((f32[128,64,128]{2,1,0:T(8,128)}), f32[128,64,128]{2,1,0:T(8,128)}, u32[]{:S(2)}, u32[]{:S(2)}) %all-to-all-start) | async-done | bytes 4194336 | tf_op jit(solution)/shard_map/all_to_all | solution.py:258
  87.5 0.0 copy-done.4
  87.5 0.0 copy-start.6
  87.5 14.5 %seeded.1 = f32[32,4,64,128]{3,2,1,0:T(8,128)S(1)} custom-call(f32[32,4,64,128]{3,2,1,0:T(8,128)} %bitcast.2.arr, f32[4,512,512]{2,1,0:T(8,128)} %seeds.1.seed, f32[4,512,512]{2,1,0:T(8,128)} %fusion.13.sym, bf16[6,256,256]{2,1,0:T(8,128)(2,1)S(1)} %copy-done.4), custom_call_target="tpu_custom_call" | custom-call | tf_op jit(solution)/shard_map/seeded/pallas_call | solution.py:314
  102.0 0.0 copy-start.2
  102.0 0.0 copy-start.5
  102.0 56.9 %all_to_all.25.arr = f32[128,64,128]{2,1,0:T(8,128)S(1)} all-to-all(f32[128,64,128]{2,1,0:T(8,128)S(1)} %bitcast.12), channel_id=1, replica_groups=mesh['slab_0'=4,'slab_1'=4,'slab_2'=2,'pen'=4] {'slab_0','slab_1','slab_..., dimensions={0} | all-to-all | bytes 8388608 | tf_op jit(solution)/shard_map/all_to_all | solution.py:258
  159.0 0.0 copy-done.6
  159.0 0.0 copy-done.2
  159.0 0.0 copy-done.5
  159.0 9.1 %middle.1 = (f32[16,128,512]{2,1,0:T(8,128)}, f32[128,64,128]{2,1,0:T(8,128)S(1)}) custom-call(f32[128,64,128]{2,1,0:T(8,128)S(1)} %all_to_all.25.arr, f32[16,128,512]{2,1,0:T(8,128)S(1)} %copy-done.6, f32[16,128,512]{2,1,0:T(8,128)S(1)} %copy-done.5, f32[16,128,512]{2,1,0:T(8,128)S(1)} %copy-done.2, s32[128,512]{1,0:T(8,128)S(1)} %cells.1.zmap, ...), custom_call_target="tpu_custom_call" | custom-call | tf_op jit(solution)/shard_map/middle/pallas_call | solution.py:325
  168.1 0.0 copy-start
  168.1 56.9 %all_to_all.26 = f32[128,64,128]{2,1,0:T(8,128)S(1)} all-to-all(f32[128,64,128]{2,1,0:T(8,128)S(1)} %get-tuple-element.10), channel_id=1, replica_groups=mesh['slab_0'=4,'slab_1'=4,'slab_2'=2,'pen'=4] {'slab_0','slab_1','slab_..., dimensions={0} | all-to-all | bytes 8388608 | tf_op jit(solution)/shard_map/all_to_all | solution.py:258
  225.0 0.0 copy-done
  225.0 11.3 %spectral.1 = f32[32,4,64,128]{3,2,1,0:T(8,128)S(1)} custom-call(f32[32,4,64,128]{3,2,1,0:T(8,128)S(1)} %bitcast.10, f32[4,512,512]{2,1,0:T(8,128)S(1)} %copy-done, bf16[6,256,256]{2,1,0:T(8,128)(2,1)S(1)} %copy-done.4), custom_call_target="tpu_custom_call" | custom-call | tf_op jit(solution)/shard_map/spectral/pallas_call | solution.py:314
  236.3 0.0 copy-start.7
  236.3 56.9 %all_to_all.27.arr = f32[128,64,128]{2,1,0:T(8,128)S(1)} all-to-all(f32[128,64,128]{2,1,0:T(8,128)S(1)} %bitcast.11), channel_id=1, replica_groups=mesh['slab_0'=4,'slab_1'=4,'slab_2'=2,'pen'=4] {'slab_0','slab_1','slab_..., dimensions={0} | all-to-all | bytes 8388608 | tf_op jit(solution)/shard_map/all_to_all | solution.py:258
  293.2 0.0 copy-done.7
  293.2 6.0 %last.1 = f32[16,128,512]{2,1,0:T(8,128)} custom-call(f32[128,64,128]{2,1,0:T(8,128)S(1)} %all_to_all.27.arr, f32[16,128,512]{2,1,0:T(8,128)S(1)} %copy-done.7, f32[16,128,512]{2,1,0:T(8,128)S(1)} %copy-done.5, f32[16,128,512]{2,1,0:T(8,128)S(1)} %copy-done.2, s32[128,512]{1,0:T(8,128)S(1)} %cells.1.zmap, f32[128,512]{1,0:T(8,128)S(1)} %get-tuple-element.8.vmap0, ...), custom_call_target="tpu_custom_call" | custom-call | tf_op jit(solution)/shard_map/last/pallas_call | solution.py:335
  (4 shorter events, 0.0 us)
Async XLA Ops:
  2.1 22.4 %all-to-all-start.1 = ((f32[128,1,32]{2,1,0:T(1,128)}), f32[128,1,32]{2,1,0:T(1,128)S(1)}, u32[]{:S(2)}, u32[]{:S(2)}) async-start(f32[128,1,32]{2,1,0:T(1,128)} %broadcast_in_dim.5), calls=%async_computation.1 | async-start | bytes 131072 | tf_op jit(solution)/shard_map/all_to_all | solution.py:258
  13.6 0.8 copy-start.8
  15.8 2.2 copy-start.1
  18.0 1.1 copy-start.3
  24.5 10.2 %copy-start.9 = (s32[3,2048]{1,0:T(4,128)S(1)}, s32[3,2048]{1,0:T(4,128)}, u32[]{:S(2)}) copy-start(s32[3,2048]{1,0:T(4,128)} %vox.5) | copy-start | bytes 73732
  24.5 63.1 %all-to-all-start = ((f32[128,64,128]{2,1,0:T(8,128)}), f32[128,64,128]{2,1,0:T(8,128)}, u32[]{:S(2)}, u32[]{:S(2)}) async-start(f32[128,64,128]{2,1,0:T(8,128)} %first.1), calls=%async_computation | async-start | bytes 8388608 | tf_op jit(solution)/shard_map/all_to_all | solution.py:258
  34.7 4.3 %copy-start.10 = (s32[2048]{0:T(1024)S(1)}, s32[2048]{0:T(1024)}, u32[]{:S(2)}) copy-start(s32[2048]{0:T(1024)} %param.12) | copy-start | bytes 24580
  34.9 52.6 %copy-start.4 = (bf16[6,256,256]{2,1,0:T(8,128)(2,1)S(1)}, bf16[6,256,256]{2,1,0:T(8,128)(2,1)}, u32[]{:S(2)}) copy-start(bf16[6,256,256]{2,1,0:T(8,128)(2,1)} %constant.85.clone.tab) | copy-start | bytes 2359300
  87.5 71.4 %copy-start.6 = (f32[16,128,512]{2,1,0:T(8,128)S(1)}, f32[16,128,512]{2,1,0:T(8,128)}, u32[]{:S(2)}) copy-start(f32[16,128,512]{2,1,0:T(8,128)} %prev.1) | copy-start | bytes 12582916
  102.0 56.9 %copy-start.2 = (f32[16,128,512]{2,1,0:T(8,128)S(1)}, f32[16,128,512]{2,1,0:T(8,128)}, u32[]{:S(2)}) copy-start(f32[16,128,512]{2,1,0:T(8,128)} %p.5) | copy-start | bytes 12582916
  102.0 56.9 %copy-start.5 = (f32[16,128,512]{2,1,0:T(8,128)S(1)}, f32[16,128,512]{2,1,0:T(8,128)}, u32[]{:S(2)}) copy-start(f32[16,128,512]{2,1,0:T(8,128)} %speed.3) | copy-start | bytes 12582916
  168.1 56.9 %copy-start = (f32[4,512,512]{2,1,0:T(8,128)S(1)}, f32[4,512,512]{2,1,0:T(8,128)}, u32[]{:S(2)}) copy-start(f32[4,512,512]{2,1,0:T(8,128)} %fusion.13.sym) | copy-start | bytes 12582916
  236.3 57.0 %copy-start.7 = (f32[16,128,512]{2,1,0:T(8,128)S(1)}, f32[16,128,512]{2,1,0:T(8,128)}, u32[]{:S(2)}) copy-start(f32[16,128,512]{2,1,0:T(8,128)} %get-tuple-element.6.cur) | copy-start | bytes 12582916

commit v4 on v3

--- a/solution.py
+++ b/solution.py
@@ -18,6 +18,8 @@
 SLAB_PEN = ("slab_0", "slab_1", "slab_2", "pen")
 HALF_CFL = 0.25
 MIB = 1024 * 1024
+ZB = 4
+PZ = 2
 F32 = jnp.float32
 BF16 = jnp.bfloat16
 
@@ -120,55 +122,64 @@
 
 
 def forward_x(cur, tab, out):
-    flat = cur.reshape(256, NX)
-    a, b = flat[:, :HALF], flat[:, HALF:]
-    out2 = out.reshape(1024, 128)
-    for part, (which, data) in enumerate(((EVEN, a + b), (ODD, a - b))):
-        got = dot(table3(tab, which, 1), split3(data, 1), ((1,), (1,)))
-        for k in range(2):
-            for z in range(2):
-                out2[pl.ds(z * 4 + part * 2 + k, 128, stride=8), :] = got[
-                    k * 128 : (k + 1) * 128, z * 128 : (z + 1) * 128
-                ]
+    sums = []
+    for piece in cur:
+        flat = piece.reshape(PZ * 128, NX)
+        sums.append((flat[:, :HALF] + flat[:, HALF:], flat[:, :HALF] - flat[:, HALF:]))
+    got = [
+        [dot(table3(tab, (EVEN, ODD)[part], 1), split3(pair[part], 1), ((1,), (1,))) for part in range(2)]
+        for pair in sums
+    ]
+    for i, pair in enumerate(got):
+        for part in range(2):
+            pieces = [pair[part][:, z * 128 : (z + 1) * 128].reshape(64, 4, 128) for z in range(2)]
+            out[pl.ds(part * 64, 64), pl.ds(i * 8, 8), :] = jnp.concatenate(pieces, axis=1)
 
 
 def inverse_x(arr, tab):
-    arr2 = arr.reshape(1024, 128)
     halves = []
-    for part, which in enumerate((EVEN, ODD)):
-        pieces = []
-        for z in range(2):
-            rows = [arr2[pl.ds(z * 4 + part * 2 + k, 128, stride=8), :] for k in range(2)]
-            pieces.append(jnp.concatenate(rows, axis=0))
-        data = jnp.concatenate(pieces, axis=1)
-        halves.append(dot(split3(data, 0), table3(tab, which, 0), ((0,), (0,))))
-    even, odd = halves
-    return jnp.concatenate([even + odd, even - odd], axis=1).reshape(2, 128, NX)
-
-
-def inject(base, zmap, vmap):
-    z = lax.broadcasted_iota(jnp.int32, (2, 1, 1), 0) + 2 * pl.program_id(0)
-    return jnp.where(zmap[...][None] == z, vmap[...][None], base)
+    for i in range(ZB // PZ):
+        parts = []
+        for part, which in enumerate((EVEN, ODD)):
+            block = arr[pl.ds(part * 64, 64), pl.ds(i * 8, 8), :]
+            pieces = [block[:, z * 4 : z * 4 + 4].reshape(HALF, 128) for z in range(2)]
+            data = jnp.concatenate(pieces, axis=1)
+            parts.append(dot(split3(data.T, 1), table3(tab, which, 0), ((1,), (0,))))
+        halves.append(parts)
+    return [
+        jnp.concatenate([even + odd, even - odd], axis=1).reshape(PZ, 128, NX) for even, odd in halves
+    ]
+
+
+def planes(i):
+    return pl.ds(i * PZ, PZ)
+
+
+def here(zmap, i):
+    z = lax.broadcasted_iota(jnp.int32, (PZ, 1, 1), 0) + ZB * pl.program_id(0) + i * PZ
+    return zmap[...][None] == z
 
 
 def first_kernel(p, zmap, tab, out):
-    z = lax.broadcasted_iota(jnp.int32, (2, 1, 1), 0) + 2 * pl.program_id(0)
-    forward_x(jnp.where(zmap[...][None] == z, 0.0, p[...]), tab, out)
+    forward_x([jnp.where(here(zmap, i), 0.0, p[planes(i)]) for i in range(ZB // PZ)], tab, out)
 
 
 def middle_kernel(arr, prev, speed, p, zmap, vmap0, vmap1, tab, cur_out, out):
-    update = inverse_x(arr, tab)
-    now = inject(p[...], zmap, vmap0)
-    following = 2.0 * now - prev[...] + speed[...] * update
-    cur = inject(following, zmap, vmap1)
-    cur_out[...] = cur
-    forward_x(cur, tab, out)
+    current = []
+    for i, update in enumerate(inverse_x(arr, tab)):
+        hit = here(zmap, i)
+        now = jnp.where(hit, vmap0[...][None], p[planes(i)])
+        following = 2.0 * now - prev[planes(i)] + speed[planes(i)] * update
+        cur = jnp.where(hit, vmap1[...][None], following)
+        cur_out[planes(i)] = cur
+        current.append(cur)
+    forward_x(current, tab, out)
 
 
 def last_kernel(arr, cur, speed, p, zmap, vmap0, tab, final):
-    update = inverse_x(arr, tab)
-    before = inject(p[...], zmap, vmap0)
-    final[...] = 2.0 * cur[...] - before + speed[...] * update
+    for i, update in enumerate(inverse_x(arr, tab)):
+        before = jnp.where(here(zmap, i), vmap0[...][None], p[planes(i)])
+        final[planes(i)] = 2.0 * cur[planes(i)] - before + speed[planes(i)] * update
 
 
 def seeded_kernel(arr, seed, sym, tab, out):
@@ -176,32 +187,43 @@
 
 
 def spectral_kernel(arr, sym, tab, out, seed=None):
-    k = pl.program_id(0)
-    pens = [arr[:, p, pl.ds(k, 16, stride=4), :].reshape(512, 128) for p in range(4)]
-    a = jnp.concatenate(pens[:2], axis=1)
-    b = jnp.concatenate(pens[2:], axis=1)
-    if seed is not None:
-        a = a + seed[0, :, :HALF]
-        b = b + seed[0, :, HALF:]
-    back = []
-    for part, data in enumerate((a + b, a - b)):
-        which = (EVEN, ODD_T)[part]
-        x = dot(split3(data, 1), table3(tab, which, 0), ((1,), (0,)))
+    step = pl.program_id(0)
+    by_y = []
+    for j in range(2):
+        k = step * 2 + j
+        pens = [arr[:, p, pl.ds(k, 16, stride=4), :].reshape(512, 128) for p in range(4)]
+        a = jnp.concatenate(pens[:2], axis=1)
+        b = jnp.concatenate(pens[2:], axis=1)
+        if seed is not None:
+            a = a + seed[j, :, :HALF]
+            b = b + seed[j, :, HALF:]
+        by_y += [
+            dot(split3(data, 1), table3(tab, which, 0), ((1,), (0,)))
+            for which, data in ((EVEN, a + b), (ODD_T, a - b))
+        ]
+    by_z = []
+    for x in by_y:
         top, bottom = x[:HALF], x[HALF:]
-        even = dot(table3(tab, EVEN, 1), split3(top + bottom, 0), ((1,), (0,)))
-        odd = dot(table3(tab, ODD, 1), split3(top - bottom, 0), ((1,), (0,)))
-        cols = pl.ds(part * HALF, HALF)
-        even = even * sym[0, pl.ds(0, HALF), cols]
-        odd = odd * sym[0, pl.ds(HALF, HALF), cols]
-        even = dot(table3(tab, EVEN, 1), split3(even, 0), ((1,), (0,)))
-        odd = dot(table3(tab, ODD_T, 1), split3(odd, 0), ((1,), (0,)))
+        by_z.append(dot(table3(tab, EVEN, 1), split3(top + bottom, 0), ((1,), (0,))))
+        by_z.append(dot(table3(tab, ODD, 1), split3(top - bottom, 0), ((1,), (0,))))
+    scaled = [
+        x * sym[i // 4, pl.ds(i % 2 * HALF, HALF), pl.ds(i % 4 // 2 * HALF, HALF)] for i, x in enumerate(by_z)
+    ]
+    back_z = [
+        dot(table3(tab, (EVEN, ODD_T)[i % 2], 1), split3(x, 0), ((1,), (0,)))
+        for i, x in enumerate(scaled)
+    ]
+    back_y = []
+    for part in range(4):
+        even, odd = back_z[2 * part], back_z[2 * part + 1]
         z = jnp.concatenate([even + odd, even - odd], axis=0)
-        back.append(dot(split3(z, 1), table3(tab, (EVEN, ODD)[part], 0), ((1,), (0,))))
-    a = back[0] + back[1]
-    b = back[0] - back[1]
-    for p in range(4):
-        piece = (a, b)[p // 2][:, (p % 2) * 128 : (p % 2) * 128 + 128]
-        out[:, p, pl.ds(k, 16, stride=4), :] = piece.reshape(32, 16, 128)
+        back_y.append(dot(split3(z, 1), table3(tab, (EVEN, ODD)[part % 2], 0), ((1,), (0,))))
+    for j in range(2):
+        a = back_y[2 * j] + back_y[2 * j + 1]
+        b = back_y[2 * j] - back_y[2 * j + 1]
+        for p in range(4):
+            piece = (a, b)[p // 2][:, (p % 2) * 128 : (p % 2) * 128 + 128]
+            out[:, p, pl.ds(step * 2 + j, 16, stride=4), :] = piece.reshape(32, 16, 128)
 
 
 def whole(*shape):
@@ -209,11 +231,11 @@
 
 
 def pairs():
-    return pl.BlockSpec((2, 128, NX), lambda i: (i, 0, 0))
+    return pl.BlockSpec((ZB, 128, NX), lambda i: (i, 0, 0))
 
 
 def packed():
-    return pl.BlockSpec((128, 8, 128), lambda i: (0, i, 0))
+    return pl.BlockSpec((128, 4 * ZB, 128), lambda i: (0, i, 0))
 
 
 def params(mib):
@@ -237,7 +259,7 @@
 
 
 def local_freq(device):
-    return half_order(jnp.arange(4, dtype=jnp.int32) * 128 + device)
+    return half_order(device * 4 + jnp.arange(4, dtype=jnp.int32))
 
 
 def symbol_of(device):
@@ -277,11 +299,11 @@
     )(offs, sensor_voxels)
     wire = pl.pallas_call(
         first_kernel,
-        grid=(8,),
+        grid=(16 // ZB,),
         in_specs=[pairs(), MAP, TAB],
         out_specs=packed(),
         out_shape=pltpu.HBM((128, 64, 128), F32),
-        compiler_params=params(12),
+        compiler_params=params(16),
         name="first",
     )(pressure, zmap, tab)
     arr = exchange(wire)
@@ -298,6 +320,7 @@
     angle = (local_freq(device)[:, None] * sensor_voxels[2][None, :] % NX).astype(F32) * (2.0 * math.pi / NX)
     weight = row0 * (jnp.cos(angle) + jnp.sin(angle))
     plane = pl.BlockSpec((1, 512, 512), lambda i: (i, 0, 0))
+    planes2 = pl.BlockSpec((2, 512, 512), lambda i: (i, 0, 0))
     seed = pl.pallas_call(
         seed_kernel,
         grid=(4,),
@@ -313,32 +336,32 @@
         symbol = pltpu.with_memory_space_constraint(sym, pltpu.HBM) if extra else sym
         return pl.pallas_call(
             seeded_kernel if extra else spectral_kernel,
-            grid=(4,),
-            in_specs=[whole(32, 4, 64, 128)] + [plane] * (len(extra) + 1) + [TAB],
+            grid=(2,),
+            in_specs=[whole(32, 4, 64, 128)] + [planes2] * (len(extra) + 1) + [TAB],
             out_specs=whole(32, 4, 64, 128),
             out_shape=jax.ShapeDtypeStruct((32, 4, 64, 128), F32),
-            compiler_params=params(24),
+            compiler_params=params(32),
             name="seeded" if extra else "spectral",
         )(arr.reshape(32, 4, 64, 128), *extra, symbol, tab).reshape(128, 64, 128)
 
     arr = exchange(spectral(arr, pltpu.with_memory_space_constraint(seed, pltpu.HBM)))
     current, wire = pl.pallas_call(
         middle_kernel,
-        grid=(8,),
+        grid=(16 // ZB,),
         in_specs=[packed(), pairs(), pairs(), pairs(), MAP, MAP, MAP, TAB],
         out_specs=(pairs(), packed()),
         out_shape=(GRID, WIRE),
-        compiler_params=params(16),
+        compiler_params=params(24),
         name="middle",
     )(arr, previous, speed_ratio, pressure, zmap, vmap0, vmap1, tab)
     arr = exchange(spectral(exchange(wire)))
     final = pl.pallas_call(
         last_kernel,
-        grid=(8,),
+        grid=(16 // ZB,),
         in_specs=[packed(), pairs(), pairs(), pairs(), MAP, MAP, TAB],
         out_specs=pairs(),
         out_shape=GRID,
-        compiler_params=params(16),
+        compiler_params=params(24),
         name="last",
     )(arr, current, speed_ratio, pressure, zmap, vmap0, tab)
     return (final, current)

time: 300 us -> 288 us (0.960)
  Pallas kernels: 60.6 us -> 48.5 us
    pallas_call x5, Pallas kernels: 46.2 us -> 34.1 us  [the longest x2 18.8 us: spectral(): pl.pallas_call(seeded_kernel if extra else spectral_kernel, grid=(2,), in...]
  transfers between devices with their start and end apart: 2 -> 2, of which waited for: 1 -> 2; matrix products, arithmetic and copies ran while one was open for 2% -> 2% of each run, Pallas kernels for 7% -> 6%
where the time goes in v4:
time: 288 us; the launch traced here: 287 us
  blocking collectives  171 us (59%)
  Pallas kernels  48.5 us (17%)
  waiting for transfers between devices  35.3 us (12%)
  starting transfers between devices  21.5 us (7%)
  local copies, waits for them, and re-layouts  5.55 us (2%)
  other arithmetic  4.69 us (2%)
    all_to_all x3, blocking collectives, exchange(): lax.all_to_all(array, SLAB_PEN, split_axis=0, concat_axis=0, tiled=True)  171 us
    all_to_all x2, waiting for transfers between devices, exchange(): lax.all_to_all(array, SLAB_PEN, split_axis=0, concat_axis=0, tiled=True)  35.3 us
    all_to_all x2, starting transfers between devices, exchange(): lax.all_to_all(array, SLAB_PEN, split_axis=0, concat_axis=0, tiled=True)  21.5 us
    pallas_call x2, Pallas kernels, spectral(): pl.pallas_call(seeded_kernel if extra else spectral_kernel, grid=(2,), in...  18.8 us
    pallas_call x1, Pallas kernels, step_pair(): pl.pallas_call(seed_kernel, grid=(4,), in_specs=[whole(3, SENSORS), whole...  10.5 us
    pallas_call x1, Pallas kernels, step_pair(): pl.pallas_call(middle_kernel, grid=(16 // ZB,), in_specs=[packed(), pairs...  6.92 us
  transfers between devices with their start and end apart: 2, of which 2 were waited for; matrix products, arithmetic and copies ran while one was open for 2% of the time, Pallas kernels for 6%

profile of v4, /device:TPU:1, one launch (start us, length us, event | category | flops | bytes accessed | tf_op | source)
XLA Modules:
  0.0 287.1 jit_solution(11160877248239984732)
XLA Ops:
  0.6 0.8 broadcast_in_dim.4
  1.4 0.7 broadcast_in_dim.5
  2.1 11.5 %all-to-all-start.1 = ((f32[128,1,32]{2,1,0:T(1,128)}), f32[128,1,32]{2,1,0:T(1,128)S(1)}, u32[]{:S(2)}, u32[]{:S(2)}) async-start(f32[128,1,32]{2,1,0:T(1,128)} %broadcast_in_dim.5), calls=%async_computation.1 | async-start | bytes 131072 | tf_op jit(solution)/shard_map/all_to_all | solution.py:280
  13.6 0.1 pad_add_fusion.offs
  13.6 0.0 copy-start.8
  13.6 0.8 copy-done.8
  14.4 1.4 cells.1.zmap
  15.8 0.0 copy-start.1
  15.8 2.2 copy-done.1
  18.0 0.0 copy-start.3
  18.0 1.1 copy-done.3
  19.1 3.9 %first.1 = f32[128,64,128]{2,1,0:T(8,128)} custom-call(f32[16,128,512]{2,1,0:T(8,128)S(1)} %copy-done.1, s32[128,512]{1,0:T(8,128)S(1)} %cells.1.zmap, bf16[6,256,256]{2,1,0:T(8,128)(2,1)S(1)} %copy-done.3), custom_call_target="tpu_custom_call" | custom-call | tf_op jit(solution)/shard_map/first/pallas_call | solution.py:300
  23.0 0.0 copy-start.9
  23.0 0.2 all-to-all-done.1
  23.1 10.0 %all-to-all-start = ((f32[128,64,128]{2,1,0:T(8,128)}), f32[128,64,128]{2,1,0:T(8,128)}, u32[]{:S(2)}, u32[]{:S(2)}) async-start(f32[128,64,128]{2,1,0:T(8,128)} %first.1), calls=%async_computation | async-start | bytes 8388608 | tf_op jit(solution)/shard_map/all_to_all | solution.py:280
  33.2 0.0 copy-done.9
  33.2 0.0 copy-start.10
  33.3 0.1 broadcast_add_fusion
  33.4 0.0 copy-start.4
  33.4 4.1 %fusion.13.sym = f32[4,512,512]{2,1,0:T(8,128)} fusion(f32[4]{0:T(128)S(1)} %multiply_multiply_fusion.1, f32[512,512]{1,0:T(8,128)S(1)} %broadcast_add_fusion), kind=kLoop, calls=%fused_computation.16 | loop fusion | flops 19922944 | bytes 5242896 | tf_op jit(solution)/shard_map/mul | solution.py:276
  37.5 0.0 copy-done.10
  37.5 2.5 values.1
  40.1 0.3 add_multiply_fusion.2.weight
  40.4 10.5 %seeds.1.seed = f32[4,512,512]{2,1,0:T(8,128)} custom-call(s32[3,2048]{1,0:T(4,128)S(1)} %copy-done.9, f32[4,2048]{1,0:T(4,128)S(1)} %add_multiply_fusion.2.weight), custom_call_target="tpu_custom_call" | custom-call | tf_op jit(solution)/shard_map/seeds/pallas_call | solution.py:324
  50.9 35.1 %all-to-all-done = f32[128,64,128]{2,1,0:T(8,128)} async-done(((f32[128,64,128]{2,1,0:T(8,128)}), f32[128,64,128]{2,1,0:T(8,128)}, u32[]{:S(2)}, u32[]{:S(2)}) %all-to-all-start) | async-done | bytes 4194336 | tf_op jit(solution)/shard_map/all_to_all | solution.py:280
  86.0 0.0 copy-done.4
  86.0 0.0 copy-start.6
  86.0 11.3 %seeded.1 = f32[32,4,64,128]{3,2,1,0:T(8,128)S(1)} custom-call(f32[32,4,64,128]{3,2,1,0:T(8,128)} %bitcast.2.arr, f32[4,512,512]{2,1,0:T(8,128)} %seeds.1.seed, f32[4,512,512]{2,1,0:T(8,128)} %fusion.13.sym, bf16[6,256,256]{2,1,0:T(8,128)(2,1)S(1)} %copy-done.4), custom_call_target="tpu_custom_call" | custom-call | tf_op jit(solution)/shard_map/seeded/pallas_call | solution.py:337
  97.3 0.0 copy-start.2
  97.3 0.0 copy-start.5
  97.3 56.9 %all_to_all.25.arr = f32[128,64,128]{2,1,0:T(8,128)S(1)} all-to-all(f32[128,64,128]{2,1,0:T(8,128)S(1)} %bitcast.12), channel_id=1, replica_groups=mesh['slab_0'=4,'slab_1'=4,'slab_2'=2,'pen'=4] {'slab_0','slab_1','slab_..., dimensions={0} | all-to-all | bytes 8388608 | tf_op jit(solution)/shard_map/all_to_all | solution.py:280
  154.3 0.0 copy-done.6
  154.3 0.0 copy-done.2
  154.3 0.0 copy-done.5
  154.3 6.9 %middle.1 = (f32[16,128,512]{2,1,0:T(8,128)}, f32[128,64,128]{2,1,0:T(8,128)S(1)}) custom-call(f32[128,64,128]{2,1,0:T(8,128)S(1)} %all_to_all.25.arr, f32[16,128,512]{2,1,0:T(8,128)S(1)} %copy-done.6, f32[16,128,512]{2,1,0:T(8,128)S(1)} %copy-done.5, f32[16,128,512]{2,1,0:T(8,128)S(1)} %copy-done.2, s32[128,512]{1,0:T(8,128)S(1)} %cells.1.zmap, ...), custom_call_target="tpu_custom_call" | custom-call | tf_op jit(solution)/shard_map/middle/pallas_call | solution.py:348
  161.2 0.0 copy-start
  161.2 56.9 %all_to_all.26 = f32[128,64,128]{2,1,0:T(8,128)S(1)} all-to-all(f32[128,64,128]{2,1,0:T(8,128)S(1)} %get-tuple-element.10), channel_id=1, replica_groups=mesh['slab_0'=4,'slab_1'=4,'slab_2'=2,'pen'=4] {'slab_0','slab_1','slab_..., dimensions={0} | all-to-all | bytes 8388608 | tf_op jit(solution)/shard_map/all_to_all | solution.py:280
  218.1 0.0 copy-done
  218.1 7.5 %spectral.1 = f32[32,4,64,128]{3,2,1,0:T(8,128)S(1)} custom-call(f32[32,4,64,128]{3,2,1,0:T(8,128)S(1)} %bitcast.10, f32[4,512,512]{2,1,0:T(8,128)S(1)} %copy-done, bf16[6,256,256]{2,1,0:T(8,128)(2,1)S(1)} %copy-done.4), custom_call_target="tpu_custom_call" | custom-call | tf_op jit(solution)/shard_map/spectral/pallas_call | solution.py:337
  225.6 0.0 copy-start.7
  225.7 56.9 %all_to_all.27.arr = f32[128,64,128]{2,1,0:T(8,128)S(1)} all-to-all(f32[128,64,128]{2,1,0:T(8,128)S(1)} %bitcast.11), channel_id=1, replica_groups=mesh['slab_0'=4,'slab_1'=4,'slab_2'=2,'pen'=4] {'slab_0','slab_1','slab_..., dimensions={0} | all-to-all | bytes 8388608 | tf_op jit(solution)/shard_map/all_to_all | solution.py:280
  282.6 0.0 copy-done.7
  282.6 4.5 %last.1 = f32[16,128,512]{2,1,0:T(8,128)} custom-call(f32[128,64,128]{2,1,0:T(8,128)S(1)} %all_to_all.27.arr, f32[16,128,512]{2,1,0:T(8,128)S(1)} %copy-done.7, f32[16,128,512]{2,1,0:T(8,128)S(1)} %copy-done.5, f32[16,128,512]{2,1,0:T(8,128)S(1)} %copy-done.2, s32[128,512]{1,0:T(8,128)S(1)} %cells.1.zmap, f32[128,512]{1,0:T(8,128)S(1)} %get-tuple-element.8.vmap0, ...), custom_call_target="tpu_custom_call" | custom-call | tf_op jit(solution)/shard_map/last/pallas_call | solution.py:358
  (4 shorter events, 0.0 us)
Async XLA Ops:
  2.1 21.1 %all-to-all-start.1 = ((f32[128,1,32]{2,1,0:T(1,128)}), f32[128,1,32]{2,1,0:T(1,128)S(1)}, u32[]{:S(2)}, u32[]{:S(2)}) async-start(f32[128,1,32]{2,1,0:T(1,128)} %broadcast_in_dim.5), calls=%async_computation.1 | async-start | bytes 131072 | tf_op jit(solution)/shard_map/all_to_all | solution.py:280
  13.6 0.8 copy-start.8
  15.8 2.2 copy-start.1
  18.0 1.1 copy-start.3
  23.0 10.2 %copy-start.9 = (s32[3,2048]{1,0:T(4,128)S(1)}, s32[3,2048]{1,0:T(4,128)}, u32[]{:S(2)}) copy-start(s32[3,2048]{1,0:T(4,128)} %vox.5) | copy-start | bytes 73732
  23.1 62.9 %all-to-all-start = ((f32[128,64,128]{2,1,0:T(8,128)}), f32[128,64,128]{2,1,0:T(8,128)}, u32[]{:S(2)}, u32[]{:S(2)}) async-start(f32[128,64,128]{2,1,0:T(8,128)} %first.1), calls=%async_computation | async-start | bytes 8388608 | tf_op jit(solution)/shard_map/all_to_all | solution.py:280
  33.2 4.3 %copy-start.10 = (s32[2048]{0:T(1024)S(1)}, s32[2048]{0:T(1024)}, u32[]{:S(2)}) copy-start(s32[2048]{0:T(1024)} %param.12) | copy-start | bytes 24580
  33.4 52.6 %copy-start.4 = (bf16[6,256,256]{2,1,0:T(8,128)(2,1)S(1)}, bf16[6,256,256]{2,1,0:T(8,128)(2,1)}, u32[]{:S(2)}) copy-start(bf16[6,256,256]{2,1,0:T(8,128)(2,1)} %constant.84.clone.tab) | copy-start | bytes 2359300
  86.0 68.2 %copy-start.6 = (f32[16,128,512]{2,1,0:T(8,128)S(1)}, f32[16,128,512]{2,1,0:T(8,128)}, u32[]{:S(2)}) copy-start(f32[16,128,512]{2,1,0:T(8,128)} %prev.1) | copy-start | bytes 12582916
  97.3 56.9 %copy-start.2 = (f32[16,128,512]{2,1,0:T(8,128)S(1)}, f32[16,128,512]{2,1,0:T(8,128)}, u32[]{:S(2)}) copy-start(f32[16,128,512]{2,1,0:T(8,128)} %p.5) | copy-start | bytes 12582916
  97.3 56.9 %copy-start.5 = (f32[16,128,512]{2,1,0:T(8,128)S(1)}, f32[16,128,512]{2,1,0:T(8,128)}, u32[]{:S(2)}) copy-start(f32[16,128,512]{2,1,0:T(8,128)} %speed.3) | copy-start | bytes 12582916
  161.2 56.9 %copy-start = (f32[4,512,512]{2,1,0:T(8,128)S(1)}, f32[4,512,512]{2,1,0:T(8,128)}, u32[]{:S(2)}) copy-start(f32[4,512,512]{2,1,0:T(8,128)} %fusion.13.sym) | copy-start | bytes 12582916
  225.6 56.9 %copy-start.7 = (f32[16,128,512]{2,1,0:T(8,128)S(1)}, f32[16,128,512]{2,1,0:T(8,128)}, u32[]{:S(2)}) copy-start(f32[16,128,512]{2,1,0:T(8,128)} %get-tuple-element.6.cur) | copy-start | bytes 12582916

commit v5 on v4

--- a/solution.py
+++ b/solution.py
@@ -63,7 +63,8 @@
     return lax.dot_general(left, right, (dims, ((), ())), preferred_element_type=F32)
 
 
-def cell_kernel(offs, vox, zmap):
+def cell_kernel(offs, vox, traces, zmap, spread):
+    spread[...] = jnp.broadcast_to(traces[...][None], (128, 2, 16))
     z = vox[0:1, :] - offs[0]
     y = vox[1:2, :] - offs[1]
     inside = (z >= 0) & (z < 16) & (y >= 0) & (y < 128)
@@ -109,7 +110,27 @@
     vmap1[...] = out[384:512] + out[512:640] + out[640:768]
 
 
-def seed_kernel(vox, weight, out):
+def to_y(a, b, tab):
+    return [
+        dot(split3(data, 1), table3(tab, which, 0), ((1,), (0,)))
+        for which, data in ((EVEN, a + b), (ODD_T, a - b))
+    ]
+
+
+def to_z(by_y, tab):
+    by_z = []
+    for x in by_y:
+        top, bottom = x[:HALF], x[HALF:]
+        by_z.append(dot(table3(tab, EVEN, 1), split3(top + bottom, 0), ((1,), (0,))))
+        by_z.append(dot(table3(tab, ODD, 1), split3(top - bottom, 0), ((1,), (0,))))
+    return by_z
+
+
+def quarter(i):
+    return pl.ds(i % 2 * HALF, HALF), pl.ds(i // 2 * HALF, HALF)
+
+
+def seed_kernel(vox, weight, tab, out):
     rows = lax.broadcasted_iota(jnp.int32, (512, SENSORS), 0)
     onrow = rows == vox[0:1, :]
     oncol = (rows == vox[1:2, :]).astype(F32).astype(BF16)
@@ -118,7 +139,10 @@
     low = value - high
     lhs = [jnp.where(onrow, part, 0.0).astype(BF16) for part in (high, low)]
     got = dot(jnp.concatenate(lhs, axis=0), oncol, ((1,), (1,)))
-    out[0] = got[:512] + got[512:]
+    got = got[:512] + got[512:]
+    for i, x in enumerate(to_z(to_y(got[:, :HALF], got[:, HALF:], tab), tab)):
+        rows_of, cols_of = quarter(i)
+        out[0, rows_of, cols_of] = x
 
 
 def forward_x(cur, tab, out):
@@ -182,33 +206,51 @@
         final[planes(i)] = 2.0 * cur[planes(i)] - before + speed[planes(i)] * update
 
 
-def seeded_kernel(arr, seed, sym, tab, out):
-    spectral_kernel(arr, sym, tab, out, seed)
-
-
-def spectral_kernel(arr, sym, tab, out, seed=None):
+def seeded_kernel(arr, seed, sym, tab, out, seed_v, sym_v, sems):
     step = pl.program_id(0)
+
+    def copy(which, h):
+        src, dst = ((seed, seed_v), (sym, sym_v))[which]
+        planes_of = pl.ds(2 * h, 2)
+        return pltpu.make_async_copy(src.at[planes_of], dst.at[planes_of], sems.at[which, h])
+
+    @pl.when(step == 0)
+    def _():
+        for h in range(2):
+            copy(0, h).start()
+            copy(1, h).start()
+
+    by_z = analyse(arr, tab, step)
+    copy(0, step).wait()
+    copy(1, step).wait()
+    for j in range(2):
+        for i in range(4):
+            rows_of, cols_of = quarter(i)
+            k = 2 * step + j
+            by_z[4 * j + i] = (by_z[4 * j + i] + seed_v[k, rows_of, cols_of]) * sym_v[k, rows_of, cols_of]
+    synthesise(by_z, tab, out, step)
+
+
+def spectral_kernel(arr, sym, tab, out):
+    step = pl.program_id(0)
+    by_z = analyse(arr, tab, step)
+    for j in range(2):
+        for i in range(4):
+            rows_of, cols_of = quarter(i)
+            by_z[4 * j + i] = by_z[4 * j + i] * sym[j, rows_of, cols_of]
+    synthesise(by_z, tab, out, step)
+
+
+def analyse(arr, tab, step):
     by_y = []
     for j in range(2):
         k = step * 2 + j
         pens = [arr[:, p, pl.ds(k, 16, stride=4), :].reshape(512, 128) for p in range(4)]
-        a = jnp.concatenate(pens[:2], axis=1)
-        b = jnp.concatenate(pens[2:], axis=1)
-        if seed is not None:
-            a = a + seed[j, :, :HALF]
-            b = b + seed[j, :, HALF:]
-        by_y += [
-            dot(split3(data, 1), table3(tab, which, 0), ((1,), (0,)))
-            for which, data in ((EVEN, a + b), (ODD_T, a - b))
-        ]
-    by_z = []
-    for x in by_y:
-        top, bottom = x[:HALF], x[HALF:]
-        by_z.append(dot(table3(tab, EVEN, 1), split3(top + bottom, 0), ((1,), (0,))))
-        by_z.append(dot(table3(tab, ODD, 1), split3(top - bottom, 0), ((1,), (0,))))
-    scaled = [
-        x * sym[i // 4, pl.ds(i % 2 * HALF, HALF), pl.ds(i % 4 // 2 * HALF, HALF)] for i, x in enumerate(by_z)
-    ]
+        by_y += to_y(jnp.concatenate(pens[:2], axis=1), jnp.concatenate(pens[2:], axis=1), tab)
+    return to_z(by_y, tab)
+
+
+def synthesise(scaled, tab, out, step):
     back_z = [
         dot(table3(tab, (EVEN, ODD_T)[i % 2], 1), split3(x, 0), ((1,), (0,)))
         for i, x in enumerate(scaled)
@@ -276,6 +318,10 @@
     return square * ratio * ratio * scale
 
 
+def in_hbm(array):
+    return pltpu.with_memory_space_constraint(array, pltpu.HBM)
+
+
 def exchange(array):
     return lax.all_to_all(array, SLAB_PEN, split_axis=0, concat_axis=0, tiled=True)
 
@@ -288,15 +334,18 @@
     offs = jnp.stack([slab_index * 16, pen_index * 128]).astype(jnp.int32)
     in_smem = pl.BlockSpec(memory_space=pltpu.SMEM)
     in_vmem = pl.BlockSpec(memory_space=pltpu.VMEM)
-    gathered = exchange(jnp.broadcast_to(traces.reshape(1, 1, 32), (128, 1, 32)))
-    zmap = pl.pallas_call(
+    zmap, copies = pl.pallas_call(
         cell_kernel,
-        in_specs=[in_smem, in_vmem],
-        out_specs=in_vmem,
-        out_shape=jax.ShapeDtypeStruct((128, NX), jnp.int32),
+        in_specs=[in_smem, in_vmem, in_vmem],
+        out_specs=(in_vmem, in_vmem),
+        out_shape=(
+            jax.ShapeDtypeStruct((128, NX), jnp.int32),
+            jax.ShapeDtypeStruct((128, 2, 16), F32),
+        ),
         compiler_params=params(8),
         name="cells",
-    )(offs, sensor_voxels)
+    )(offs, sensor_voxels, traces)
+    gathered = exchange(copies)
     wire = pl.pallas_call(
         first_kernel,
         grid=(16 // ZB,),
@@ -305,7 +354,7 @@
         out_shape=pltpu.HBM((128, 64, 128), F32),
         compiler_params=params(16),
         name="first",
-    )(pressure, zmap, tab)
+    )(in_hbm(pressure), zmap, in_hbm(tab))
     arr = exchange(wire)
 
     map_type = jax.ShapeDtypeStruct((128, NX), F32)
@@ -324,27 +373,32 @@
     seed = pl.pallas_call(
         seed_kernel,
         grid=(4,),
-        in_specs=[whole(3, SENSORS), whole(4, SENSORS)],
+        in_specs=[whole(3, SENSORS), whole(4, SENSORS), TAB],
         out_specs=plane,
         out_shape=pltpu.HBM((4, 512, 512), F32),
         compiler_params=params(12),
         name="seeds",
-    )(sensor_voxels, weight)
+    )(sensor_voxels, weight, tab)
     sym = symbol_of(device)
 
-    def spectral(arr, *extra):
-        symbol = pltpu.with_memory_space_constraint(sym, pltpu.HBM) if extra else sym
-        return pl.pallas_call(
-            seeded_kernel if extra else spectral_kernel,
-            grid=(2,),
-            in_specs=[whole(32, 4, 64, 128)] + [planes2] * (len(extra) + 1) + [TAB],
-            out_specs=whole(32, 4, 64, 128),
-            out_shape=jax.ShapeDtypeStruct((32, 4, 64, 128), F32),
-            compiler_params=params(32),
-            name="seeded" if extra else "spectral",
-        )(arr.reshape(32, 4, 64, 128), *extra, symbol, tab).reshape(128, 64, 128)
-
-    arr = exchange(spectral(arr, pltpu.with_memory_space_constraint(seed, pltpu.HBM)))
+    cube = whole(32, 4, 64, 128)
+    cube_type = jax.ShapeDtypeStruct((32, 4, 64, 128), F32)
+    raw = pl.BlockSpec(memory_space=pl.ANY)
+    arr = pl.pallas_call(
+        seeded_kernel,
+        grid=(2,),
+        in_specs=[cube, raw, raw, TAB],
+        out_specs=cube,
+        out_shape=cube_type,
+        scratch_shapes=[
+            pltpu.VMEM((4, 512, 512), F32),
+            pltpu.VMEM((4, 512, 512), F32),
+            pltpu.SemaphoreType.DMA((2, 2)),
+        ],
+        compiler_params=params(32),
+        name="seeded",
+    )(arr.reshape(32, 4, 64, 128), in_hbm(seed), in_hbm(sym), tab)
+    arr = exchange(arr.reshape(128, 64, 128))
     current, wire = pl.pallas_call(
         middle_kernel,
         grid=(16 // ZB,),
@@ -354,7 +408,16 @@
         compiler_params=params(24),
         name="middle",
     )(arr, previous, speed_ratio, pressure, zmap, vmap0, vmap1, tab)
-    arr = exchange(spectral(exchange(wire)))
+    arr = pl.pallas_call(
+        spectral_kernel,
+        grid=(2,),
+        in_specs=[cube, planes2, TAB],
+        out_specs=cube,
+        out_shape=cube_type,
+        compiler_params=params(24),
+        name="spectral",
+    )(exchange(wire).reshape(32, 4, 64, 128), sym, tab)
+    arr = exchange(arr.reshape(128, 64, 128))
     final = pl.pallas_call(
         last_kernel,
         grid=(16 // ZB,),

time: 288 us -> 287 us (level)
  Pallas kernels: 48.5 us -> 56 us
  local copies, waits for them, and re-layouts: 5.55 us -> 1.66 us
  starting transfers between devices: 21.5 us -> 18 us
    pallas_call x1, Pallas kernels: 10.5 us -> 14.4 us  [step_pair(): pl.pallas_call(seed_kernel, grid=(4,), in_specs=[whole(3, SENSORS), whole...]
    all_to_all x2, starting transfers between devices: 21.5 us -> 18 us  [exchange(): lax.all_to_all(array, SLAB_PEN, split_axis=0, concat_axis=0, tiled=True)]
  transfers between devices with their start and end apart: 2 -> 2, of which waited for: 2 -> 2; matrix products, arithmetic and copies ran while one was open for 2% -> 2% of each run, Pallas kernels for 6% -> 8%
where the time goes in v5:
time: 287 us
  blocking collectives  171 us (60%)
  Pallas kernels  56 us (20%)
  waiting for transfers between devices  34.7 us (12%)
  starting transfers between devices  18 us (6%)
  other arithmetic  4.69 us (2%)
    all_to_all x3, blocking collectives, exchange(): lax.all_to_all(array, SLAB_PEN, split_axis=0, concat_axis=0, tiled=True)  171 us
    all_to_all x2, waiting for transfers between devices, exchange(): lax.all_to_all(array, SLAB_PEN, split_axis=0, concat_axis=0, tiled=True)  34.7 us
    all_to_all x2, starting transfers between devices, exchange(): lax.all_to_all(array, SLAB_PEN, split_axis=0, concat_axis=0, tiled=True)  18 us
    pallas_call x1, Pallas kernels, step_pair(): pl.pallas_call(seed_kernel, grid=(4,), in_specs=[whole(3, SENSORS), whole...  14.4 us
    pallas_call x1, Pallas kernels, step_pair(): pl.pallas_call(seeded_kernel, grid=(2,), in_specs=[cube, raw, raw, TAB],...  11.5 us
    pallas_call x1, Pallas kernels, step_pair(): pl.pallas_call(spectral_kernel, grid=(2,), in_specs=[cube, planes2, TAB],...  7.53 us
    pallas_call x1, Pallas kernels, step_pair(): pl.pallas_call(middle_kernel, grid=(16 // ZB,), in_specs=[packed(), pairs...  7.21 us
    pallas_call x1, Pallas kernels, step_pair(): pl.pallas_call(first_kernel, grid=(16 // ZB,), in_specs=[pairs(), MAP, TA...  6.08 us
  transfers between devices with their start and end apart: 2, of which 2 were waited for; matrix products, arithmetic and copies ran while one was open for 2% of the time, Pallas kernels for 8%

profile of v5, /device:TPU:1, one launch (start us, length us, event | category | flops | bytes accessed | tf_op | source)
XLA Modules:
  0.0 286.5 jit_solution(1839348093382710903)
XLA Ops:
  0.6 0.1 pad_add_fusion.offs
  0.7 0.0 copy-start.6
  0.7 0.8 copy-done.6
  1.5 0.0 copy-start.9
  1.5 0.7 copy-done.9
  2.2 1.9 cells.1
  4.1 11.5 %all-to-all-start.1 = ((f32[128,2,16]{2,1,0:T(2,128)}), f32[128,2,16]{2,1,0:T(2,128)S(1)}, u32[]{:S(2)}, u32[]{:S(2)}) async-start(f32[128,2,16]{2,1,0:T(2,128)} %get-tuple-element.10), calls=%async_computation.1 | async-start | bytes 262144 | tf_op jit(solution)/shard_map/all_to_all | solution.py:326
  15.6 6.1 %first.1 = f32[128,64,128]{2,1,0:T(8,128)} custom-call(f32[16,128,512]{2,1,0:T(8,128)} %p.5, s32[128,512]{1,0:T(8,128)S(1)} %get-tuple-element.9.zmap, bf16[6,256,256]{2,1,0:T(8,128)(2,1)} %constant.84.clone.tab), custom_call_target="tpu_custom_call" | custom-call | tf_op jit(solution)/shard_map/first/pallas_call | solution.py:349
  21.7 0.0 copy-start.7
  21.7 3.7 %all-to-all-done.1 = f32[128,2,16]{2,1,0:T(2,128)S(1)} async-done(((f32[128,2,16]{2,1,0:T(2,128)}), f32[128,2,16]{2,1,0:T(2,128)S(1)}, u32[]{:S(2)}, u32[]{:S(2)}) %all-to-all-start.1) | async-done | bytes 16416 | tf_op jit(solution)/shard_map/all_to_all | solution.py:326
  25.4 6.5 %all-to-all-start = ((f32[128,64,128]{2,1,0:T(8,128)}), f32[128,64,128]{2,1,0:T(8,128)}, u32[]{:S(2)}, u32[]{:S(2)}) async-start(f32[128,64,128]{2,1,0:T(8,128)} %first.1), calls=%async_computation | async-start | bytes 8388608 | tf_op jit(solution)/shard_map/all_to_all | solution.py:326
  31.9 0.0 copy-done.7
  31.9 0.0 copy-start.8
  31.9 0.0 copy-start.2
  32.0 0.1 broadcast_add_fusion
  32.2 4.1 %fusion.13.sym = f32[4,512,512]{2,1,0:T(8,128)} fusion(f32[4]{0:T(128)S(1)} %multiply_multiply_fusion.1, f32[512,512]{1,0:T(8,128)S(1)} %broadcast_add_fusion), kind=kLoop, calls=%fused_computation.16 | loop fusion | flops 19922944 | bytes 5242896 | tf_op jit(solution)/shard_map/mul | solution.py:318
  36.3 0.1 copy.9
  36.3 0.1 copy.10.gathered
  36.4 0.0 copy-done.8
  36.4 2.5 values.1
  39.0 0.3 add_multiply_fusion.2.weight
  39.3 0.0 copy-done.2
  39.3 14.4 %seeds.1.seed = f32[4,512,512]{2,1,0:T(8,128)} custom-call(s32[3,2048]{1,0:T(4,128)S(1)} %copy-done.7, f32[4,2048]{1,0:T(4,128)S(1)} %add_multiply_fusion.2.weight, bf16[6,256,256]{2,1,0:T(8,128)(2,1)S(1)} %copy-done.2), custom_call_target="tpu_custom_call" | custom-call | tf_op jit(solution)/shard_map/seeds/pallas_call | solution.py:373
  53.8 31.0 %all-to-all-done = f32[128,64,128]{2,1,0:T(8,128)} async-done(((f32[128,64,128]{2,1,0:T(8,128)}), f32[128,64,128]{2,1,0:T(8,128)}, u32[]{:S(2)}, u32[]{:S(2)}) %all-to-all-start) | async-done | bytes 4194336 | tf_op jit(solution)/shard_map/all_to_all | solution.py:326
  84.7 0.0 copy-start.4
  84.7 11.5 %seeded.1 = f32[32,4,64,128]{3,2,1,0:T(8,128)S(1)} custom-call(f32[32,4,64,128]{3,2,1,0:T(8,128)} %bitcast.2.arr, f32[4,512,512]{2,1,0:T(8,128)} %seeds.1.seed, f32[4,512,512]{2,1,0:T(8,128)} %fusion.13.sym, bf16[6,256,256]{2,1,0:T(8,128)(2,1)S(1)} %copy-done.2), custom_call_target="tpu_custom_call" | custom-call | tf_op jit(solution)/shard_map/seeded/pallas_call | solution.py:387
  96.3 0.0 copy-start.1
  96.3 0.0 copy-start.3
  96.3 56.9 %all_to_all.25.arr = f32[128,64,128]{2,1,0:T(8,128)S(1)} all-to-all(f32[128,64,128]{2,1,0:T(8,128)S(1)} %bitcast.12), channel_id=1, replica_groups=mesh['slab_0'=4,'slab_1'=4,'slab_2'=2,'pen'=4] {'slab_0','slab_1','slab_..., dimensions={0} | all-to-all | bytes 8388608 | tf_op jit(solution)/shard_map/all_to_all | solution.py:326
  153.2 0.0 copy-done.4
  153.2 0.0 copy-done.1
  153.2 0.0 copy-done.3
  153.2 7.2 %middle.1 = (f32[16,128,512]{2,1,0:T(8,128)}, f32[128,64,128]{2,1,0:T(8,128)S(1)}) custom-call(f32[128,64,128]{2,1,0:T(8,128)S(1)} %all_to_all.25.arr, f32[16,128,512]{2,1,0:T(8,128)S(1)} %copy-done.4, f32[16,128,512]{2,1,0:T(8,128)S(1)} %copy-done.3, f32[16,128,512]{2,1,0:T(8,128)S(1)} %copy-done.1, s32[128,512]{1,0:T(8,128)S(1)} %get-tuple-element.9.zmap, ...), custom_call_target="tpu_custom_call" | custom-call | tf_op jit(solution)/shard_map/middle/pallas_call | solution.py:402
  160.4 0.0 copy-start
  160.4 56.9 %all_to_all.26 = f32[128,64,128]{2,1,0:T(8,128)S(1)} all-to-all(f32[128,64,128]{2,1,0:T(8,128)S(1)} %get-tuple-element.14), channel_id=1, replica_groups=mesh['slab_0'=4,'slab_1'=4,'slab_2'=2,'pen'=4] {'slab_0','slab_1','slab_..., dimensions={0} | all-to-all | bytes 8388608 | tf_op jit(solution)/shard_map/all_to_all | solution.py:326
  217.3 0.0 copy-done
  217.3 7.5 %spectral.1 = f32[32,4,64,128]{3,2,1,0:T(8,128)S(1)} custom-call(f32[32,4,64,128]{3,2,1,0:T(8,128)S(1)} %bitcast.10, f32[4,512,512]{2,1,0:T(8,128)S(1)} %copy-done, bf16[6,256,256]{2,1,0:T(8,128)(2,1)S(1)} %copy-done.2), custom_call_target="tpu_custom_call" | custom-call | tf_op jit(solution)/shard_map/spectral/pallas_call | solution.py:411
  224.9 0.0 copy-start.5
  224.9 56.9 %all_to_all.27.arr = f32[128,64,128]{2,1,0:T(8,128)S(1)} all-to-all(f32[128,64,128]{2,1,0:T(8,128)S(1)} %bitcast.11), channel_id=1, replica_groups=mesh['slab_0'=4,'slab_1'=4,'slab_2'=2,'pen'=4] {'slab_0','slab_1','slab_..., dimensions={0} | all-to-all | bytes 8388608 | tf_op jit(solution)/shard_map/all_to_all | solution.py:326
  281.8 0.0 copy-done.5
  281.8 4.7 %last.1 = f32[16,128,512]{2,1,0:T(8,128)} custom-call(f32[128,64,128]{2,1,0:T(8,128)S(1)} %all_to_all.27.arr, f32[16,128,512]{2,1,0:T(8,128)S(1)} %copy-done.5, f32[16,128,512]{2,1,0:T(8,128)S(1)} %copy-done.3, f32[16,128,512]{2,1,0:T(8,128)S(1)} %copy-done.1, s32[128,512]{1,0:T(8,128)S(1)} %get-tuple-element.9.zmap, ...), custom_call_target="tpu_custom_call" | custom-call | tf_op jit(solution)/shard_map/last/pallas_call | solution.py:421
  (4 shorter events, 0.0 us)
Async XLA Ops:
  0.7 0.8 copy-start.6
  1.5 0.7 copy-start.9
  4.1 21.3 %all-to-all-start.1 = ((f32[128,2,16]{2,1,0:T(2,128)}), f32[128,2,16]{2,1,0:T(2,128)S(1)}, u32[]{:S(2)}, u32[]{:S(2)}) async-start(f32[128,2,16]{2,1,0:T(2,128)} %get-tuple-element.10), calls=%async_computation.1 | async-start | bytes 262144 | tf_op jit(solution)/shard_map/all_to_all | solution.py:326
  21.7 10.2 %copy-start.7 = (s32[3,2048]{1,0:T(4,128)S(1)}, s32[3,2048]{1,0:T(4,128)}, u32[]{:S(2)}) copy-start(s32[3,2048]{1,0:T(4,128)} %vox.5) | copy-start | bytes 73732
  25.4 59.3 %all-to-all-start = ((f32[128,64,128]{2,1,0:T(8,128)}), f32[128,64,128]{2,1,0:T(8,128)}, u32[]{:S(2)}, u32[]{:S(2)}) async-start(f32[128,64,128]{2,1,0:T(8,128)} %first.1), calls=%async_computation | async-start | bytes 8388608 | tf_op jit(solution)/shard_map/all_to_all | solution.py:326
  31.9 4.5 %copy-start.8 = (s32[2048]{0:T(1024)S(1)}, s32[2048]{0:T(1024)}, u32[]{:S(2)}) copy-start(s32[2048]{0:T(1024)} %param.12) | copy-start | bytes 24580
  31.9 7.4 %copy-start.2 = (bf16[6,256,256]{2,1,0:T(8,128)(2,1)S(1)}, bf16[6,256,256]{2,1,0:T(8,128)(2,1)}, u32[]{:S(2)}) copy-start(bf16[6,256,256]{2,1,0:T(8,128)(2,1)} %constant.84.clone.tab) | copy-start | bytes 2359300
  84.7 68.5 %copy-start.4 = (f32[16,128,512]{2,1,0:T(8,128)S(1)}, f32[16,128,512]{2,1,0:T(8,128)}, u32[]{:S(2)}) copy-start(f32[16,128,512]{2,1,0:T(8,128)} %prev.1) | copy-start | bytes 12582916
  96.3 57.0 %copy-start.1 = (f32[16,128,512]{2,1,0:T(8,128)S(1)}, f32[16,128,512]{2,1,0:T(8,128)}, u32[]{:S(2)}) copy-start(f32[16,128,512]{2,1,0:T(8,128)} %p.5) | copy-start | bytes 12582916
  96.3 56.9 %copy-start.3 = (f32[16,128,512]{2,1,0:T(8,128)S(1)}, f32[16,128,512]{2,1,0:T(8,128)}, u32[]{:S(2)}) copy-start(f32[16,128,512]{2,1,0:T(8,128)} %speed.3) | copy-start | bytes 12582916
  160.4 56.9 %copy-start = (f32[4,512,512]{2,1,0:T(8,128)S(1)}, f32[4,512,512]{2,1,0:T(8,128)}, u32[]{:S(2)}) copy-start(f32[4,512,512]{2,1,0:T(8,128)} %fusion.13.sym) | copy-start | bytes 12582916
  224.9 56.9 %copy-start.5 = (f32[16,128,512]{2,1,0:T(8,128)S(1)}, f32[16,128,512]{2,1,0:T(8,128)}, u32[]{:S(2)}) copy-start(f32[16,128,512]{2,1,0:T(8,128)} %get-tuple-element.8.cur) | copy-start | bytes 12582916

commit v6 on v5

--- a/solution.py
+++ b/solution.py
@@ -63,20 +63,7 @@
     return lax.dot_general(left, right, (dims, ((), ())), preferred_element_type=F32)
 
 
-def cell_kernel(offs, vox, traces, zmap, spread):
-    spread[...] = jnp.broadcast_to(traces[...][None], (128, 2, 16))
-    z = vox[0:1, :] - offs[0]
-    y = vox[1:2, :] - offs[1]
-    inside = (z >= 0) & (z < 16) & (y >= 0) & (y < 128)
-    y = jnp.where(inside, y, -1)
-    rows128 = lax.broadcasted_iota(jnp.int32, (128, SENSORS), 0)
-    lhs = jnp.where(rows128 == y, (z + 1).astype(F32), 0.0).astype(BF16)
-    columns = lax.broadcasted_iota(jnp.int32, (NX, SENSORS), 0)
-    oncol = (columns == vox[2:3, :]).astype(F32).astype(BF16)
-    zmap[...] = dot(lhs, oncol, ((1,), (1,))).astype(jnp.int32) - 1
-
-
-def value_kernel(offs, vox, tcol, gathered, vmap0, vmap1, row0):
+def fill_maps(offs, vox, tcol, gathered, zmap, vmap0, vmap1):
     z = vox[0:1, :] - offs[0]
     y = vox[1:2, :] - offs[1]
     tile = tcol[...] // 16
@@ -93,11 +80,9 @@
     rows16 = lax.broadcasted_iota(jnp.int32, (16, SENSORS), 0)
     here = rows16 == lane
     onrow = rows128 == y
-    lhs = []
+    lhs = [jnp.where(onrow, (z + 1).astype(F32), 0.0).astype(BF16)]
     for t in range(2):
         value = jnp.sum(jnp.where(here, spread[16 * t : 16 * t + 16], 0.0), axis=0, keepdims=True)
-        if t == 0:
-            row0[...] = value
         v0 = value.astype(BF16).astype(F32)
         v1 = (value - v0).astype(BF16).astype(F32)
         v2 = value - v0 - v1
@@ -106,8 +91,9 @@
     columns = lax.broadcasted_iota(jnp.int32, (NX, SENSORS), 0)
     oncol = (columns == vox[2:3, :]).astype(F32).astype(BF16)
     out = dot(jnp.concatenate(lhs, axis=0), oncol, ((1,), (1,)))
-    vmap0[...] = out[0:128] + out[128:256] + out[256:384]
-    vmap1[...] = out[384:512] + out[512:640] + out[640:768]
+    zmap[...] = out[0:128].astype(jnp.int32) - 1
+    vmap0[...] = out[128:256] + out[256:384] + out[384:512]
+    vmap1[...] = out[512:640] + out[640:768] + out[768:896]
 
 
 def to_y(a, b, tab):
@@ -128,21 +114,6 @@
 
 def quarter(i):
     return pl.ds(i % 2 * HALF, HALF), pl.ds(i // 2 * HALF, HALF)
-
-
-def seed_kernel(vox, weight, tab, out):
-    rows = lax.broadcasted_iota(jnp.int32, (512, SENSORS), 0)
-    onrow = rows == vox[0:1, :]
-    oncol = (rows == vox[1:2, :]).astype(F32).astype(BF16)
-    value = weight[pl.ds(pl.program_id(0), 1), :]
-    high = value.astype(BF16).astype(F32)
-    low = value - high
-    lhs = [jnp.where(onrow, part, 0.0).astype(BF16) for part in (high, low)]
-    got = dot(jnp.concatenate(lhs, axis=0), oncol, ((1,), (1,)))
-    got = got[:512] + got[512:]
-    for i, x in enumerate(to_z(to_y(got[:, :HALF], got[:, HALF:], tab), tab)):
-        rows_of, cols_of = quarter(i)
-        out[0, rows_of, cols_of] = x
 
 
 def forward_x(cur, tab, out):
@@ -184,8 +155,14 @@
     return zmap[...][None] == z
 
 
-def first_kernel(p, zmap, tab, out):
-    forward_x([jnp.where(here(zmap, i), 0.0, p[planes(i)]) for i in range(ZB // PZ)], tab, out)
+def first_kernel(offs, vox, tcol, gathered, p, tab, zmap, vmap0, vmap1, out):
+    @pl.when(pl.program_id(0) == 0)
+    def _():
+        fill_maps(offs, vox, tcol, gathered, zmap, vmap0, vmap1)
+
+    forward_x(
+        [jnp.where(here(zmap, i), vmap0[...][None], p[planes(i)]) for i in range(ZB // PZ)], tab, out
+    )
 
 
 def middle_kernel(arr, prev, speed, p, zmap, vmap0, vmap1, tab, cur_out, out):
@@ -204,31 +181,6 @@
     for i, update in enumerate(inverse_x(arr, tab)):
         before = jnp.where(here(zmap, i), vmap0[...][None], p[planes(i)])
         final[planes(i)] = 2.0 * cur[planes(i)] - before + speed[planes(i)] * update
-
-
-def seeded_kernel(arr, seed, sym, tab, out, seed_v, sym_v, sems):
-    step = pl.program_id(0)
-
-    def copy(which, h):
-        src, dst = ((seed, seed_v), (sym, sym_v))[which]
-        planes_of = pl.ds(2 * h, 2)
-        return pltpu.make_async_copy(src.at[planes_of], dst.at[planes_of], sems.at[which, h])
-
-    @pl.when(step == 0)
-    def _():
-        for h in range(2):
-            copy(0, h).start()
-            copy(1, h).start()
-
-    by_z = analyse(arr, tab, step)
-    copy(0, step).wait()
-    copy(1, step).wait()
-    for j in range(2):
-        for i in range(4):
-            rows_of, cols_of = quarter(i)
-            k = 2 * step + j
-            by_z[4 * j + i] = (by_z[4 * j + i] + seed_v[k, rows_of, cols_of]) * sym_v[k, rows_of, cols_of]
-    synthesise(by_z, tab, out, step)
 
 
 def spectral_kernel(arr, sym, tab, out):
@@ -332,73 +284,41 @@
     device = slab_index * 4 + pen_index
     tab = jnp.asarray(half_tables())
     offs = jnp.stack([slab_index * 16, pen_index * 128]).astype(jnp.int32)
+    gathered = exchange(jnp.broadcast_to(traces[None], (128, 2, 16)))
+    sym = symbol_of(device)
     in_smem = pl.BlockSpec(memory_space=pltpu.SMEM)
-    in_vmem = pl.BlockSpec(memory_space=pltpu.VMEM)
-    zmap, copies = pl.pallas_call(
-        cell_kernel,
-        in_specs=[in_smem, in_vmem, in_vmem],
-        out_specs=(in_vmem, in_vmem),
-        out_shape=(
-            jax.ShapeDtypeStruct((128, NX), jnp.int32),
-            jax.ShapeDtypeStruct((128, 2, 16), F32),
-        ),
-        compiler_params=params(8),
-        name="cells",
-    )(offs, sensor_voxels, traces)
-    gathered = exchange(copies)
-    wire = pl.pallas_call(
+    map_type = jax.ShapeDtypeStruct((128, NX), F32)
+    zmap, vmap0, vmap1, wire = pl.pallas_call(
         first_kernel,
         grid=(16 // ZB,),
-        in_specs=[pairs(), MAP, TAB],
-        out_specs=packed(),
-        out_shape=pltpu.HBM((128, 64, 128), F32),
-        compiler_params=params(16),
+        in_specs=[in_smem, whole(3, SENSORS), whole(1, SENSORS), whole(128, 32), pairs(), TAB],
+        out_specs=(MAP, MAP, MAP, packed()),
+        out_shape=(jax.ShapeDtypeStruct((128, NX), jnp.int32), map_type, map_type, WIRE),
+        compiler_params=params(24),
         name="first",
-    )(in_hbm(pressure), zmap, in_hbm(tab))
-    arr = exchange(wire)
-
-    map_type = jax.ShapeDtypeStruct((128, NX), F32)
-    vmap0, vmap1, row0 = pl.pallas_call(
-        value_kernel,
-        in_specs=[in_smem] + [in_vmem] * 3,
-        out_specs=(in_vmem,) * 3,
-        out_shape=(map_type, map_type, jax.ShapeDtypeStruct((1, SENSORS), F32)),
-        compiler_params=params(16),
-        name="values",
-    )(offs, sensor_voxels, trace_column.reshape(1, SENSORS), gathered.reshape(128, 32))
-    angle = (local_freq(device)[:, None] * sensor_voxels[2][None, :] % NX).astype(F32) * (2.0 * math.pi / NX)
-    weight = row0 * (jnp.cos(angle) + jnp.sin(angle))
-    plane = pl.BlockSpec((1, 512, 512), lambda i: (i, 0, 0))
+    )(
+        offs,
+        sensor_voxels,
+        trace_column.reshape(1, SENSORS),
+        gathered.reshape(128, 32),
+        in_hbm(pressure),
+        tab,
+    )
+    cube = whole(32, 4, 64, 128)
     planes2 = pl.BlockSpec((2, 512, 512), lambda i: (i, 0, 0))
-    seed = pl.pallas_call(
-        seed_kernel,
-        grid=(4,),
-        in_specs=[whole(3, SENSORS), whole(4, SENSORS), TAB],
-        out_specs=plane,
-        out_shape=pltpu.HBM((4, 512, 512), F32),
-        compiler_params=params(12),
-        name="seeds",
-    )(sensor_voxels, weight, tab)
-    sym = symbol_of(device)
-
-    cube = whole(32, 4, 64, 128)
-    cube_type = jax.ShapeDtypeStruct((32, 4, 64, 128), F32)
-    raw = pl.BlockSpec(memory_space=pl.ANY)
-    arr = pl.pallas_call(
-        seeded_kernel,
-        grid=(2,),
-        in_specs=[cube, raw, raw, TAB],
-        out_specs=cube,
-        out_shape=cube_type,
-        scratch_shapes=[
-            pltpu.VMEM((4, 512, 512), F32),
-            pltpu.VMEM((4, 512, 512), F32),
-            pltpu.SemaphoreType.DMA((2, 2)),
-        ],
-        compiler_params=params(32),
-        name="seeded",
-    )(arr.reshape(32, 4, 64, 128), in_hbm(seed), in_hbm(sym), tab)
-    arr = exchange(arr.reshape(128, 64, 128))
+
+    def spectral(arr):
+        return pl.pallas_call(
+            spectral_kernel,
+            grid=(2,),
+            in_specs=[cube, planes2, TAB],
+            out_specs=cube,
+            out_shape=jax.ShapeDtypeStruct((32, 4, 64, 128), F32),
+            compiler_params=params(24),
+            name="spectral",
+        )(arr.reshape(32, 4, 64, 128), sym, tab).reshape(128, 64, 128)
+
+    arr = exchange(spectral(exchange(wire)))
     current, wire = pl.pallas_call(
         middle_kernel,
         grid=(16 // ZB,),
@@ -408,16 +328,7 @@
         compiler_params=params(24),
         name="middle",
     )(arr, previous, speed_ratio, pressure, zmap, vmap0, vmap1, tab)
-    arr = pl.pallas_call(
-        spectral_kernel,
-        grid=(2,),
-        in_specs=[cube, planes2, TAB],
-        out_specs=cube,
-        out_shape=cube_type,
-        compiler_params=params(24),
-        name="spectral",
-    )(exchange(wire).reshape(32, 4, 64, 128), sym, tab)
-    arr = exchange(arr.reshape(128, 64, 128))
+    arr = exchange(spectral(exchange(wire)))
     final = pl.pallas_call(
         last_kernel,
         grid=(16 // ZB,),

time: 287 us -> 296 us (1.031)
  waiting for transfers between devices: 34.7 us -> 58.4 us
  Pallas kernels: 56 us -> 35.7 us
  local copies, waits for them, and re-layouts: 1.66 us -> 8.35 us
    all_to_all x2, waiting for transfers between devices: 34.7 us -> 58.4 us  [exchange(): lax.all_to_all(array, SLAB_PEN, split_axis=0, concat_axis=0, tiled=True)]
    pallas_call x6 -> x3, Pallas kernels: 44 us -> 24.5 us  [the longest x2 17.4 us: spectral(): pl.pallas_call(spectral_kernel, grid=(2,), in_specs=[cube, planes2, TAB],...]
    unnamed x20 -> x22, local copies, waits for them, and re-layouts: 1.48 us -> 6.82 us
  transfers between devices with their start and end apart: 2 -> 2, of which waited for: 2 -> 2; matrix products, arithmetic and copies ran while one was open for 2% -> 1% of each run, Pallas kernels for 8% -> 0%
where the time goes in v6:
time: 296 us; the launch traced here: 295 us
  blocking collectives  171 us (58%)
  waiting for transfers between devices  58.4 us (20%)
  Pallas kernels  35.7 us (12%)
  starting transfers between devices  16.7 us (6%)
  local copies, waits for them, and re-layouts  8.35 us (3%)
  other arithmetic  4.33 us (1%)
    all_to_all x3, blocking collectives, exchange(): lax.all_to_all(array, SLAB_PEN, split_axis=0, concat_axis=0, tiled=True)  171 us
    all_to_all x2, waiting for transfers between devices, exchange(): lax.all_to_all(array, SLAB_PEN, split_axis=0, concat_axis=0, tiled=True)  58.4 us
    pallas_call x2, Pallas kernels, spectral(): pl.pallas_call(spectral_kernel, grid=(2,), in_specs=[cube, planes2, TAB],...  17.4 us
    all_to_all x2, starting transfers between devices, exchange(): lax.all_to_all(array, SLAB_PEN, split_axis=0, concat_axis=0, tiled=True)  16.7 us
    pallas_call x1, Pallas kernels, step_pair(): pl.pallas_call(first_kernel, grid=(16 // ZB,), in_specs=[in_smem, whole(3...  7.12 us
    unnamed x22, local copies, waits for them, and re-layouts  6.82 us
    pallas_call x1, Pallas kernels, step_pair(): pl.pallas_call(middle_kernel, grid=(16 // ZB,), in_specs=[packed(), pairs...  6.63 us
  transfers between devices with their start and end apart: 2, of which 2 were waited for; matrix products, arithmetic and copies ran while one was open for 1% of the time, Pallas kernels for 0%

profile of v6, /device:TPU:1, one launch (start us, length us, event | category | flops | bytes accessed | tf_op | source)
XLA Modules:
  0.0 295.1 jit_solution(1382755559199088195)
XLA Ops:
  0.6 1.4 broadcast_in_dim.2
  2.0 11.5 %all-to-all-start = ((f32[128,2,16]{2,1,0:T(2,128)}), f32[128,2,16]{2,1,0:T(2,128)S(1)}, u32[]{:S(2)}, u32[]{:S(2)}) async-start(f32[128,2,16]{2,1,0:T(2,128)} %broadcast_in_dim.2), calls=%async_computation | async-start | bytes 262144 | tf_op jit(solution)/shard_map/all_to_all | solution.py:278
  13.5 0.1 pad_add_fusion.offs
  13.6 9.7 %all-to-all-done = f32[128,2,16]{2,1,0:T(2,128)S(1)} async-done(((f32[128,2,16]{2,1,0:T(2,128)}), f32[128,2,16]{2,1,0:T(2,128)S(1)}, u32[]{:S(2)}, u32[]{:S(2)}) %all-to-all-start) | async-done | bytes 16416 | tf_op jit(solution)/shard_map/all_to_all | solution.py:278
  23.3 0.1 copy.10
  23.4 0.1 copy.11.gathered
  23.5 0.0 copy-start.3
  23.5 1.1 copy-done.3
  24.6 0.0 copy-start.9
  24.6 0.8 copy-done.9
  25.4 0.0 copy-start.10
  25.4 0.7 copy-done.10
  26.1 7.1 %first.1 = (s32[128,512]{1,0:T(8,128)S(1)}, f32[128,512]{1,0:T(8,128)S(1)}, f32[128,512]{1,0:T(8,128)S(1)}, f32[128,64,128]{2,1,0:T(8,128)S(1)}) custom-call(s32[2]{0:T(128)S(1)} %pad_add_fusion.offs, s32[3,2048]{1,0:T(4,128)S(1)} %copy-done.9, s32[1,2048]{1,0:T(1,128)S(1)} %bitcast.11, f32[128,32]{1,0:T(8,128)S(1)} %copy.11.gathered, f32[16,128,512]{2,1,0:T(8,128)} %p.5, ...), custom_call_target="tpu_custom_call" | custom-call | tf_op jit(solution)/shard_map/first/pallas_call | solution.py:291
  33.2 0.0 copy-start.6
  33.2 2.0 copy-done.6
  35.2 5.2 %all-to-all-start.1 = ((f32[128,64,128]{2,1,0:T(8,128)}), f32[128,64,128]{2,1,0:T(8,128)}, u32[]{:S(2)}, u32[]{:S(2)}) async-start(f32[128,64,128]{2,1,0:T(8,128)} %copy-done.6), calls=%async_computation.1 | async-start | bytes 8388608 | tf_op jit(solution)/shard_map/all_to_all | solution.py:278
  40.5 0.0 copy-start.4
  40.5 0.1 broadcast_add_fusion
  40.7 4.1 %fusion.13.sym = f32[4,512,512]{2,1,0:T(8,128)} fusion(f32[4]{0:T(128)S(1)} %multiply_multiply_fusion.1, f32[512,512]{1,0:T(8,128)S(1)} %broadcast_add_fusion), kind=kLoop, calls=%fused_computation.16 | loop fusion | flops 19922944 | bytes 5242896 | tf_op jit(solution)/shard_map/mul | solution.py:270
  44.8 48.7 %all-to-all-done.1 = f32[128,64,128]{2,1,0:T(8,128)} async-done(((f32[128,64,128]{2,1,0:T(8,128)}), f32[128,64,128]{2,1,0:T(8,128)}, u32[]{:S(2)}, u32[]{:S(2)}) %all-to-all-start.1) | async-done | bytes 4194336 | tf_op jit(solution)/shard_map/all_to_all | solution.py:278
  93.4 0.0 copy-done.4
  93.4 0.0 copy-start
  93.4 2.2 copy-done
  95.6 0.0 copy-start.7
  95.6 9.9 %spectral.2 = f32[32,4,64,128]{3,2,1,0:T(8,128)S(1)} custom-call(f32[32,4,64,128]{3,2,1,0:T(8,128)} %bitcast.4.arr, f32[4,512,512]{2,1,0:T(8,128)S(1)} %copy-done, bf16[6,256,256]{2,1,0:T(8,128)(2,1)S(1)} %copy-done.4), custom_call_target="tpu_custom_call" | custom-call | tf_op jit(solution)/shard_map/spectral/pallas_call | solution.py:311
  105.5 0.0 copy-start.2
  105.5 0.0 copy-start.5
  105.5 56.9 %all_to_all.25.arr = f32[128,64,128]{2,1,0:T(8,128)S(1)} all-to-all(f32[128,64,128]{2,1,0:T(8,128)S(1)} %bitcast.10), channel_id=1, replica_groups=mesh['slab_0'=4,'slab_1'=4,'slab_2'=2,'pen'=4] {'slab_0','slab_1','slab_..., dimensions={0} | all-to-all | bytes 8388608 | tf_op jit(solution)/shard_map/all_to_all | solution.py:278
  162.5 0.0 copy-done.7
  162.5 0.0 copy-done.2
  162.5 0.0 copy-done.5
  162.5 6.6 %middle.1 = (f32[16,128,512]{2,1,0:T(8,128)}, f32[128,64,128]{2,1,0:T(8,128)S(1)}) custom-call(f32[128,64,128]{2,1,0:T(8,128)S(1)} %all_to_all.25.arr, f32[16,128,512]{2,1,0:T(8,128)S(1)} %copy-done.7, f32[16,128,512]{2,1,0:T(8,128)S(1)} %copy-done.5, f32[16,128,512]{2,1,0:T(8,128)S(1)} %copy-done.2, s32[128,512]{1,0:T(8,128)S(1)} %get-tuple-element.9.zmap, ...), custom_call_target="tpu_custom_call" | custom-call | tf_op jit(solution)/shard_map/middle/pallas_call | solution.py:322
  169.1 0.0 copy-start.1
  169.1 56.9 %all_to_all.26 = f32[128,64,128]{2,1,0:T(8,128)S(1)} all-to-all(f32[128,64,128]{2,1,0:T(8,128)S(1)} %get-tuple-element.12), channel_id=1, replica_groups=mesh['slab_0'=4,'slab_1'=4,'slab_2'=2,'pen'=4] {'slab_0','slab_1','slab_..., dimensions={0} | all-to-all | bytes 8388608 | tf_op jit(solution)/shard_map/all_to_all | solution.py:278
  226.0 0.0 copy-done.1
  226.0 7.5 %spectral.3 = f32[32,4,64,128]{3,2,1,0:T(8,128)S(1)} custom-call(f32[32,4,64,128]{3,2,1,0:T(8,128)S(1)} %bitcast.8, f32[4,512,512]{2,1,0:T(8,128)S(1)} %copy-done.1, bf16[6,256,256]{2,1,0:T(8,128)(2,1)S(1)} %copy-done.4), custom_call_target="tpu_custom_call" | custom-call | tf_op jit(solution)/shard_map/spectral/pallas_call | solution.py:311
  233.6 0.0 copy-start.8
  233.6 56.9 %all_to_all.27.arr = f32[128,64,128]{2,1,0:T(8,128)S(1)} all-to-all(f32[128,64,128]{2,1,0:T(8,128)S(1)} %bitcast.9), channel_id=1, replica_groups=mesh['slab_0'=4,'slab_1'=4,'slab_2'=2,'pen'=4] {'slab_0','slab_1','slab_..., dimensions={0} | all-to-all | bytes 8388608 | tf_op jit(solution)/shard_map/all_to_all | solution.py:278
  290.5 0.0 copy-done.8
  290.5 4.5 %last.1 = f32[16,128,512]{2,1,0:T(8,128)} custom-call(f32[128,64,128]{2,1,0:T(8,128)S(1)} %all_to_all.27.arr, f32[16,128,512]{2,1,0:T(8,128)S(1)} %copy-done.8, f32[16,128,512]{2,1,0:T(8,128)S(1)} %copy-done.5, f32[16,128,512]{2,1,0:T(8,128)S(1)} %copy-done.2, s32[128,512]{1,0:T(8,128)S(1)} %get-tuple-element.9.zmap, ...), custom_call_target="tpu_custom_call" | custom-call | tf_op jit(solution)/shard_map/last/pallas_call | solution.py:332
  (2 shorter events, 0.0 us)
Async XLA Ops:
  2.0 21.3 %all-to-all-start = ((f32[128,2,16]{2,1,0:T(2,128)}), f32[128,2,16]{2,1,0:T(2,128)S(1)}, u32[]{:S(2)}, u32[]{:S(2)}) async-start(f32[128,2,16]{2,1,0:T(2,128)} %broadcast_in_dim.2), calls=%async_computation | async-start | bytes 262144 | tf_op jit(solution)/shard_map/all_to_all | solution.py:278
  23.5 1.1 copy-start.3
  24.6 0.8 copy-start.9
  25.4 0.7 copy-start.10
  33.2 2.0 copy-start.6
  35.2 58.2 %all-to-all-start.1 = ((f32[128,64,128]{2,1,0:T(8,128)}), f32[128,64,128]{2,1,0:T(8,128)}, u32[]{:S(2)}, u32[]{:S(2)}) async-start(f32[128,64,128]{2,1,0:T(8,128)} %copy-done.6), calls=%async_computation.1 | async-start | bytes 8388608 | tf_op jit(solution)/shard_map/all_to_all | solution.py:278
  40.5 53.0 %copy-start.4 = (bf16[6,256,256]{2,1,0:T(8,128)(2,1)S(1)}, bf16[6,256,256]{2,1,0:T(8,128)(2,1)}, u32[]{:S(2)}) copy-start(bf16[6,256,256]{2,1,0:T(8,128)(2,1)} %constant.69.clone.tab) | copy-start | bytes 2359300
  93.4 2.2 copy-start
  95.6 66.8 %copy-start.7 = (f32[16,128,512]{2,1,0:T(8,128)S(1)}, f32[16,128,512]{2,1,0:T(8,128)}, u32[]{:S(2)}) copy-start(f32[16,128,512]{2,1,0:T(8,128)} %prev.1) | copy-start | bytes 12582916
  105.5 57.0 %copy-start.2 = (f32[16,128,512]{2,1,0:T(8,128)S(1)}, f32[16,128,512]{2,1,0:T(8,128)}, u32[]{:S(2)}) copy-start(f32[16,128,512]{2,1,0:T(8,128)} %p.5) | copy-start | bytes 12582916
  105.5 57.0 %copy-start.5 = (f32[16,128,512]{2,1,0:T(8,128)S(1)}, f32[16,128,512]{2,1,0:T(8,128)}, u32[]{:S(2)}) copy-start(f32[16,128,512]{2,1,0:T(8,128)} %speed.3) | copy-start | bytes 12582916
  169.1 56.9 %copy-start.1 = (f32[4,512,512]{2,1,0:T(8,128)S(1)}, f32[4,512,512]{2,1,0:T(8,128)}, u32[]{:S(2)}) copy-start(f32[4,512,512]{2,1,0:T(8,128)} %fusion.13.sym) | copy-start | bytes 12582916
  233.6 56.9 %copy-start.8 = (f32[16,128,512]{2,1,0:T(8,128)S(1)}, f32[16,128,512]{2,1,0:T(8,128)}, u32[]{:S(2)}) copy-start(f32[16,128,512]{2,1,0:T(8,128)} %get-tuple-element.7.cur) | copy-start | bytes 12582916

commit v7 on v6

--- a/solution.py
+++ b/solution.py
@@ -155,13 +155,28 @@
     return zmap[...][None] == z
 
 
-def first_kernel(offs, vox, tcol, gathered, p, tab, zmap, vmap0, vmap1, out):
-    @pl.when(pl.program_id(0) == 0)
+def first_kernel(offs, vox, tcol, gathered, p, tab, zmap, vmap0, vmap1, out, p_v, sems):
+    step = pl.program_id(0)
+
+    def copy(i):
+        part = pl.ds(i * ZB, ZB)
+        return pltpu.make_async_copy(p.at[part], p_v.at[part], sems.at[i])
+
+    @pl.when(step == 0)
     def _():
+        for i in range(16 // ZB):
+            copy(i).start()
         fill_maps(offs, vox, tcol, gathered, zmap, vmap0, vmap1)
 
+    copy(step).wait()
+    base = step * ZB
     forward_x(
-        [jnp.where(here(zmap, i), vmap0[...][None], p[planes(i)]) for i in range(ZB // PZ)], tab, out
+        [
+            jnp.where(here(zmap, i), vmap0[...][None], p_v[pl.ds(base + i * PZ, PZ)])
+            for i in range(ZB // PZ)
+        ],
+        tab,
+        out,
     )
 
 
@@ -291,9 +306,10 @@
     zmap, vmap0, vmap1, wire = pl.pallas_call(
         first_kernel,
         grid=(16 // ZB,),
-        in_specs=[in_smem, whole(3, SENSORS), whole(1, SENSORS), whole(128, 32), pairs(), TAB],
+        in_specs=[in_smem, whole(3, SENSORS), whole(1, SENSORS), whole(128, 32), pl.BlockSpec(memory_space=pl.ANY), TAB],
         out_specs=(MAP, MAP, MAP, packed()),
         out_shape=(jax.ShapeDtypeStruct((128, NX), jnp.int32), map_type, map_type, WIRE),
+        scratch_shapes=[pltpu.VMEM((16, 128, NX), F32), pltpu.SemaphoreType.DMA((16 // ZB,))],
         compiler_params=params(24),
         name="first",
     )(

time: 296 us -> 294 us (level)
  no operation moved by 1% of the time
where the time goes in v7:
time: 294 us
  blocking collectives  171 us (58%)
  waiting for transfers between devices  58.4 us (20%)
  Pallas kernels  34.5 us (12%)
  starting transfers between devices  16.7 us (6%)
  local copies, waits for them, and re-layouts  8.35 us (3%)
  other arithmetic  4.33 us (1%)
    all_to_all x3, blocking collectives, exchange(): lax.all_to_all(array, SLAB_PEN, split_axis=0, concat_axis=0, tiled=True)  171 us
    all_to_all x2, waiting for transfers between devices, exchange(): lax.all_to_all(array, SLAB_PEN, split_axis=0, concat_axis=0, tiled=True)  58.4 us
    pallas_call x2, Pallas kernels, spectral(): pl.pallas_call(spectral_kernel, grid=(2,), in_specs=[cube, planes2, TAB],...  17.4 us
    all_to_all x2, starting transfers between devices, exchange(): lax.all_to_all(array, SLAB_PEN, split_axis=0, concat_axis=0, tiled=True)  16.7 us
    unnamed x22, local copies, waits for them, and re-layouts  6.82 us
    pallas_call x1, Pallas kernels, step_pair(): pl.pallas_call(middle_kernel, grid=(16 // ZB,), in_specs=[packed(), pairs...  6.62 us
    pallas_call x1, Pallas kernels, step_pair(): pl.pallas_call(first_kernel, grid=(16 // ZB,), in_specs=[in_smem, whole(3...  5.91 us
  transfers between devices with their start and end apart: 2, of which 2 were waited for; matrix products, arithmetic and copies ran while one was open for 1% of the time, Pallas kernels for 0%

profile of v7, /device:TPU:1, one launch (start us, length us, event | category | flops | bytes accessed | tf_op | source)
XLA Modules:
  0.0 293.9 jit_solution(5296033037707352908)
XLA Ops:
  0.6 1.4 broadcast_in_dim.2
  2.0 11.5 %all-to-all-start = ((f32[128,2,16]{2,1,0:T(2,128)}), f32[128,2,16]{2,1,0:T(2,128)S(1)}, u32[]{:S(2)}, u32[]{:S(2)}) async-start(f32[128,2,16]{2,1,0:T(2,128)} %broadcast_in_dim.2), calls=%async_computation | async-start | bytes 262144 | tf_op jit(solution)/shard_map/all_to_all | solution.py:293
  13.5 0.1 pad_add_fusion.offs
  13.6 9.7 %all-to-all-done = f32[128,2,16]{2,1,0:T(2,128)S(1)} async-done(((f32[128,2,16]{2,1,0:T(2,128)}), f32[128,2,16]{2,1,0:T(2,128)S(1)}, u32[]{:S(2)}, u32[]{:S(2)}) %all-to-all-start) | async-done | bytes 16416 | tf_op jit(solution)/shard_map/all_to_all | solution.py:293
  23.3 0.1 copy.10
  23.4 0.1 copy.11.gathered
  23.5 0.0 copy-start.3
  23.5 1.1 copy-done.3
  24.6 0.0 copy-start.9
  24.6 0.8 copy-done.9
  25.4 0.0 copy-start.10
  25.4 0.7 copy-done.10
  26.1 5.9 %first.1 = (s32[128,512]{1,0:T(8,128)S(1)}, f32[128,512]{1,0:T(8,128)S(1)}, f32[128,512]{1,0:T(8,128)S(1)}, f32[128,64,128]{2,1,0:T(8,128)S(1)}) custom-call(s32[2]{0:T(128)S(1)} %pad_add_fusion.offs, s32[3,2048]{1,0:T(4,128)S(1)} %copy-done.9, s32[1,2048]{1,0:T(1,128)S(1)} %bitcast.11, f32[128,32]{1,0:T(8,128)S(1)} %copy.11.gathered, f32[16,128,512]{2,1,0:T(8,128)} %p.5, ...), custom_call_target="tpu_custom_call" | custom-call | tf_op jit(solution)/shard_map/first/pallas_call | solution.py:306
  32.0 0.0 copy-start.6
  32.0 2.0 copy-done.6
  34.0 5.3 %all-to-all-start.1 = ((f32[128,64,128]{2,1,0:T(8,128)}), f32[128,64,128]{2,1,0:T(8,128)}, u32[]{:S(2)}, u32[]{:S(2)}) async-start(f32[128,64,128]{2,1,0:T(8,128)} %copy-done.6), calls=%async_computation.1 | async-start | bytes 8388608 | tf_op jit(solution)/shard_map/all_to_all | solution.py:293
  39.3 0.0 copy-start.4
  39.3 0.1 broadcast_add_fusion
  39.5 4.1 %fusion.13.sym = f32[4,512,512]{2,1,0:T(8,128)} fusion(f32[4]{0:T(128)S(1)} %multiply_multiply_fusion.1, f32[512,512]{1,0:T(8,128)S(1)} %broadcast_add_fusion), kind=kLoop, calls=%fused_computation.16 | loop fusion | flops 19922944 | bytes 5242896 | tf_op jit(solution)/shard_map/mul | solution.py:285
  43.6 48.7 %all-to-all-done.1 = f32[128,64,128]{2,1,0:T(8,128)} async-done(((f32[128,64,128]{2,1,0:T(8,128)}), f32[128,64,128]{2,1,0:T(8,128)}, u32[]{:S(2)}, u32[]{:S(2)}) %all-to-all-start.1) | async-done | bytes 4194336 | tf_op jit(solution)/shard_map/all_to_all | solution.py:293
  92.2 0.0 copy-done.4
  92.2 0.0 copy-start
  92.2 2.2 copy-done
  94.4 0.0 copy-start.7
  94.4 9.9 %spectral.2 = f32[32,4,64,128]{3,2,1,0:T(8,128)S(1)} custom-call(f32[32,4,64,128]{3,2,1,0:T(8,128)} %bitcast.4.arr, f32[4,512,512]{2,1,0:T(8,128)S(1)} %copy-done, bf16[6,256,256]{2,1,0:T(8,128)(2,1)S(1)} %copy-done.4), custom_call_target="tpu_custom_call" | custom-call | tf_op jit(solution)/shard_map/spectral/pallas_call | solution.py:327
  104.3 0.0 copy-start.2
  104.4 0.0 copy-start.5
  104.4 56.9 %all_to_all.25.arr = f32[128,64,128]{2,1,0:T(8,128)S(1)} all-to-all(f32[128,64,128]{2,1,0:T(8,128)S(1)} %bitcast.10), channel_id=1, replica_groups=mesh['slab_0'=4,'slab_1'=4,'slab_2'=2,'pen'=4] {'slab_0','slab_1','slab_..., dimensions={0} | all-to-all | bytes 8388608 | tf_op jit(solution)/shard_map/all_to_all | solution.py:293
  161.3 0.0 copy-done.7
  161.3 0.0 copy-done.2
  161.3 0.0 copy-done.5
  161.3 6.6 %middle.1 = (f32[16,128,512]{2,1,0:T(8,128)}, f32[128,64,128]{2,1,0:T(8,128)S(1)}) custom-call(f32[128,64,128]{2,1,0:T(8,128)S(1)} %all_to_all.25.arr, f32[16,128,512]{2,1,0:T(8,128)S(1)} %copy-done.7, f32[16,128,512]{2,1,0:T(8,128)S(1)} %copy-done.5, f32[16,128,512]{2,1,0:T(8,128)S(1)} %copy-done.2, s32[128,512]{1,0:T(8,128)S(1)} %get-tuple-element.9.zmap, ...), custom_call_target="tpu_custom_call" | custom-call | tf_op jit(solution)/shard_map/middle/pallas_call | solution.py:338
  167.9 0.0 copy-start.1
  167.9 56.9 %all_to_all.26 = f32[128,64,128]{2,1,0:T(8,128)S(1)} all-to-all(f32[128,64,128]{2,1,0:T(8,128)S(1)} %get-tuple-element.12), channel_id=1, replica_groups=mesh['slab_0'=4,'slab_1'=4,'slab_2'=2,'pen'=4] {'slab_0','slab_1','slab_..., dimensions={0} | all-to-all | bytes 8388608 | tf_op jit(solution)/shard_map/all_to_all | solution.py:293
  224.8 0.0 copy-done.1
  224.8 7.5 %spectral.3 = f32[32,4,64,128]{3,2,1,0:T(8,128)S(1)} custom-call(f32[32,4,64,128]{3,2,1,0:T(8,128)S(1)} %bitcast.8, f32[4,512,512]{2,1,0:T(8,128)S(1)} %copy-done.1, bf16[6,256,256]{2,1,0:T(8,128)(2,1)S(1)} %copy-done.4), custom_call_target="tpu_custom_call" | custom-call | tf_op jit(solution)/shard_map/spectral/pallas_call | solution.py:327
  232.4 0.0 copy-start.8
  232.4 56.9 %all_to_all.27.arr = f32[128,64,128]{2,1,0:T(8,128)S(1)} all-to-all(f32[128,64,128]{2,1,0:T(8,128)S(1)} %bitcast.9), channel_id=1, replica_groups=mesh['slab_0'=4,'slab_1'=4,'slab_2'=2,'pen'=4] {'slab_0','slab_1','slab_..., dimensions={0} | all-to-all | bytes 8388608 | tf_op jit(solution)/shard_map/all_to_all | solution.py:293
  289.3 0.0 copy-done.8
  289.3 4.5 %last.1 = f32[16,128,512]{2,1,0:T(8,128)} custom-call(f32[128,64,128]{2,1,0:T(8,128)S(1)} %all_to_all.27.arr, f32[16,128,512]{2,1,0:T(8,128)S(1)} %copy-done.8, f32[16,128,512]{2,1,0:T(8,128)S(1)} %copy-done.5, f32[16,128,512]{2,1,0:T(8,128)S(1)} %copy-done.2, s32[128,512]{1,0:T(8,128)S(1)} %get-tuple-element.9.zmap, ...), custom_call_target="tpu_custom_call" | custom-call | tf_op jit(solution)/shard_map/last/pallas_call | solution.py:348
  (2 shorter events, 0.0 us)
Async XLA Ops:
  2.0 21.3 %all-to-all-start = ((f32[128,2,16]{2,1,0:T(2,128)}), f32[128,2,16]{2,1,0:T(2,128)S(1)}, u32[]{:S(2)}, u32[]{:S(2)}) async-start(f32[128,2,16]{2,1,0:T(2,128)} %broadcast_in_dim.2), calls=%async_computation | async-start | bytes 262144 | tf_op jit(solution)/shard_map/all_to_all | solution.py:293
  23.5 1.1 copy-start.3
  24.6 0.8 copy-start.9
  25.4 0.7 copy-start.10
  32.0 2.0 copy-start.6
  34.0 58.2 %all-to-all-start.1 = ((f32[128,64,128]{2,1,0:T(8,128)}), f32[128,64,128]{2,1,0:T(8,128)}, u32[]{:S(2)}, u32[]{:S(2)}) async-start(f32[128,64,128]{2,1,0:T(8,128)} %copy-done.6), calls=%async_computation.1 | async-start | bytes 8388608 | tf_op jit(solution)/shard_map/all_to_all | solution.py:293
  39.3 53.0 %copy-start.4 = (bf16[6,256,256]{2,1,0:T(8,128)(2,1)S(1)}, bf16[6,256,256]{2,1,0:T(8,128)(2,1)}, u32[]{:S(2)}) copy-start(bf16[6,256,256]{2,1,0:T(8,128)(2,1)} %constant.69.clone.tab) | copy-start | bytes 2359300
  92.2 2.2 copy-start
  94.4 66.8 %copy-start.7 = (f32[16,128,512]{2,1,0:T(8,128)S(1)}, f32[16,128,512]{2,1,0:T(8,128)}, u32[]{:S(2)}) copy-start(f32[16,128,512]{2,1,0:T(8,128)} %prev.1) | copy-start | bytes 12582916
  104.3 56.9 %copy-start.2 = (f32[16,128,512]{2,1,0:T(8,128)S(1)}, f32[16,128,512]{2,1,0:T(8,128)}, u32[]{:S(2)}) copy-start(f32[16,128,512]{2,1,0:T(8,128)} %p.5) | copy-start | bytes 12582916
  104.4 56.9 %copy-start.5 = (f32[16,128,512]{2,1,0:T(8,128)S(1)}, f32[16,128,512]{2,1,0:T(8,128)}, u32[]{:S(2)}) copy-start(f32[16,128,512]{2,1,0:T(8,128)} %speed.3) | copy-start | bytes 12582916
  167.9 56.9 %copy-start.1 = (f32[4,512,512]{2,1,0:T(8,128)S(1)}, f32[4,512,512]{2,1,0:T(8,128)}, u32[]{:S(2)}) copy-start(f32[4,512,512]{2,1,0:T(8,128)} %fusion.13.sym) | copy-start | bytes 12582916
  232.4 56.9 %copy-start.8 = (f32[16,128,512]{2,1,0:T(8,128)S(1)}, f32[16,128,512]{2,1,0:T(8,128)}, u32[]{:S(2)}) copy-start(f32[16,128,512]{2,1,0:T(8,128)} %get-tuple-element.7.cur) | copy-start | bytes 12582916
